TPU v7x, 8 devices: a whole 2x2x1 slice. The times are simulated.
8 devices in a mesh: dp: 2 (over z, y), cp: 4 (over x, core).
Axes of the slice: x: 2, y: 2, z: 1, core: 2. Of those that a mesh axis runs over, the one named last changes fastest.
Arguments:
- x_seq: bfloat16 [4, 4096, 1024], P('dp', 'cp'), parts along dimension 0
- dy_seq: float32 [4, 4096, 1024], P('dp', 'cp'), parts along dimension 0
- ln1_gain: float32 [1024], replicated
- ln1_bias: float32 [1024], replicated
- ln2_gain: float32 [1024], replicated
- ln2_bias: float32 [1024], replicated
- w_qkv: bfloat16 [1024, 16, 3, 64], replicated
- b_qkv: bfloat16 [16, 3, 64], replicated
- w_out: bfloat16 [1024, 1024], replicated
- b_out: bfloat16 [1024], replicated
- w_up: bfloat16 [1024, 4096], replicated
- b_up: bfloat16 [4096], replicated
- w_down: bfloat16 [4096, 1024], replicated
- b_down: bfloat16 [1024], replicated
Outputs:
- output 1: bfloat16 [4, 4096, 1024], P('dp', 'cp'), parts along dimension 0
- output 2: float32 [4, 4096, 1024], P('dp', 'cp'), parts along dimension 0
- output 3: float32 [2048], P('dp'), parts along dimension 0
- output 4: float32 [2048], P('dp'), parts along dimension 0
- output 5: float32 [2048], P('dp'), parts along dimension 0
- output 6: float32 [2048], P('dp'), parts along dimension 0
- output 7: float32 [2048, 16, 3, 64], P('dp'), parts along dimension 0
- output 8: float32 [32, 3, 64], P('dp'), parts along dimension 0
- output 9: float32 [2048, 1024], P('dp'), parts along dimension 0
- output 10: float32 [2048], P('dp'), parts along dimension 0
- output 11: float32 [2048, 4096], P('dp'), parts along dimension 0
- output 12: float32 [8192], P('dp'), parts along dimension 0
- output 13: float32 [8192, 1024], P('dp'), parts along dimension 0
- output 14: float32 [2048], P('dp'), parts along dimension 0
There are 2 independent parts. A program takes and returns all parts, laid end to end along the dimension named above; an argument that names none is the same for every part.
All inputs are finite; a program needn't handle non-finite values.
Results may differ from a plain program's by a relative error of at most 0.0164592.
Values are sent between devices in bfloat16 or wider.
A program may use at most 1 GiB of HBM per device.

v0:
```python
import jax
import jax.numpy as jnp
from jax import lax
from jax.sharding import PartitionSpec as P

EPS = 1e-5
ROPE_BASE = 10000.0
NEG_BIG = -1e30


def layer_norm(row_vals, norm_gain, norm_shift):
    row_mean = jnp.mean(row_vals, axis=-1, keepdims=True)
    centered = row_vals - row_mean
    inv_std = lax.rsqrt(jnp.mean(centered * centered, axis=-1, keepdims=True) + EPS)
    x_norm = centered * inv_std
    return x_norm * norm_gain + norm_shift, x_norm, inv_std


def norm_backward(d_out, x_norm, inv_std, norm_gain):
    d_norm = d_out * norm_gain
    d_rows = inv_std * (d_norm - jnp.mean(d_norm, axis=-1, keepdims=True) - x_norm * jnp.mean(d_norm * x_norm, axis=-1, keepdims=True))
    return d_rows, jnp.sum(d_out * x_norm, axis=(0, 1)), jnp.sum(d_out, axis=(0, 1))


def rope_tables(positions, head_dim):
    rot_dim = head_dim // 4
    inv_freq = ROPE_BASE ** (-2.0 * jnp.arange(rot_dim // 2, dtype=jnp.float32) / rot_dim)
    angles = positions.astype(jnp.float32)[:, None] * inv_freq[None, :]
    return jnp.cos(angles), jnp.sin(angles)


def apply_rotary(head_vals, cos_t, sin_t):
    half_rot = cos_t.shape[-1]
    first_half = head_vals[..., :half_rot]
    second_half = head_vals[..., half_rot:2 * half_rot]
    cos_b = cos_t[None, :, None, :]
    sin_b = sin_t[None, :, None, :]
    return jnp.concatenate([first_half * cos_b - second_half * sin_b, second_half * cos_b + first_half * sin_b, head_vals[..., 2 * half_rot:]], axis=-1)


def exact_gelu(pre_act):
    return jax.nn.gelu(pre_act, approximate=False)


def block_scores(q_rows, k_blk, qk_scale, diag_mask):
    scores = jnp.einsum('bqhe,bkhe->bhqk', q_rows, k_blk, preferred_element_type=jnp.float32) * qk_scale
    if diag_mask is None:
        return scores
    return jnp.where(diag_mask, scores, NEG_BIG)


def fold_block(soft_state, q_rows, k_blk, v_blk, qk_scale, diag_mask):
    row_max, row_sum, out_acc = soft_state
    scores = block_scores(q_rows, k_blk, qk_scale, diag_mask)
    new_max = jnp.maximum(row_max, jnp.max(scores, axis=-1))
    attn_probs = jnp.exp(scores - new_max[..., None])
    rescale = jnp.exp(row_max - new_max)
    row_sum = row_sum * rescale + jnp.sum(attn_probs, axis=-1)
    part_out = jnp.einsum('bhqk,bkhe->bqhe', attn_probs.astype(jnp.bfloat16), v_blk, preferred_element_type=jnp.float32)
    out_acc = out_acc * jnp.swapaxes(rescale, 1, 2)[..., None] + part_out
    return new_max, row_sum, out_acc


def block_grads(q_rows, k_blk, v_blk, d_ctx_bf, log_sum, row_delta, qk_scale, diag_mask):
    scores = block_scores(q_rows, k_blk, qk_scale, diag_mask)
    attn_probs = jnp.exp(scores - log_sum[..., None])
    d_v = jnp.einsum('bhqk,bqhe->bkhe', attn_probs.astype(jnp.bfloat16), d_ctx_bf, preferred_element_type=jnp.float32)
    d_probs = jnp.einsum('bqhe,bkhe->bhqk', d_ctx_bf, v_blk, preferred_element_type=jnp.float32)
    d_scores = (attn_probs * (d_probs - row_delta[..., None]) * qk_scale).astype(jnp.bfloat16)
    d_q = jnp.einsum('bhqk,bkhe->bqhe', d_scores, k_blk, preferred_element_type=jnp.float32)
    d_k = jnp.einsum('bhqk,bqhe->bkhe', d_scores, q_rows, preferred_element_type=jnp.float32)
    return d_q, d_k, d_v


def solution(mesh):
    cp_size = mesh.shape['cp']
    shift_perm = [(sender, (sender + 1) % cp_size) for sender in range(cp_size)]
    row_spec = P('dp', 'cp', None)
    in_specs = (row_spec, row_spec) + (P(),) * 12
    out_specs = (row_spec, row_spec, P('dp'), P('dp'), P('dp'), P('dp'), P('dp', None, None, None), P('dp', None, None), P('dp', None), P('dp'), P('dp', None), P('dp'), P('dp', None), P('dp'))

    def local_layer(x_blk, dy_blk, ln1_gain, ln1_bias, ln2_gain, ln2_bias, w_qkv, b_qkv, w_out, b_out, w_up, b_up, w_down, b_down):
        batch_size, row_count, model_width = x_blk.shape
        head_count, head_dim = w_qkv.shape[1], w_qkv.shape[3]
        qk_scale = head_dim ** -0.5
        my_idx = lax.axis_index('cp')
        cos_t, sin_t = rope_tables(my_idx * row_count + jnp.arange(row_count), head_dim)
        local_pos = jnp.arange(row_count)
        diag_mask = local_pos[None, :] <= local_pos[:, None]

        x_rows = x_blk.astype(jnp.float32)
        h_attn, x_norm1, inv_std1 = layer_norm(x_rows, ln1_gain, ln1_bias)
        h_attn = h_attn.astype(jnp.bfloat16)
        qkv_rows = jnp.einsum('btd,dhce->bthce', h_attn, w_qkv, preferred_element_type=jnp.float32) + b_qkv.astype(jnp.float32)
        q_rows = apply_rotary(qkv_rows[:, :, :, 0], cos_t, sin_t).astype(jnp.bfloat16)
        k_own = apply_rotary(qkv_rows[:, :, :, 1], cos_t, sin_t).astype(jnp.bfloat16)
        v_own = qkv_rows[:, :, :, 2].astype(jnp.bfloat16)

        stat_shape = (batch_size, head_count, row_count)
        start_state = (jnp.full(stat_shape, NEG_BIG, jnp.float32), jnp.zeros(stat_shape, jnp.float32), jnp.zeros((batch_size, row_count, head_count, head_dim), jnp.float32))
        own_state = fold_block(start_state, q_rows, k_own, v_own, qk_scale, diag_mask)

        def fwd_step(step_idx, carry):
            k_cur, v_cur, soft_state = carry
            k_cur, v_cur = lax.ppermute((k_cur, v_cur), 'cp', shift_perm)
            soft_state = lax.cond(step_idx <= my_idx, lambda state_in: fold_block(state_in, q_rows, k_cur, v_cur, qk_scale, None), lambda state_in: state_in, soft_state)
            return k_cur, v_cur, soft_state

        row_max, row_sum, out_acc = lax.fori_loop(1, cp_size, fwd_step, (k_own, v_own, own_state))[2]
        attn_norm = out_acc / jnp.swapaxes(row_sum, 1, 2)[..., None]
        log_sum = row_max + jnp.log(row_sum)
        attn_ctx = attn_norm.astype(jnp.bfloat16).reshape(batch_size, row_count, model_width)
        attn_proj = jnp.einsum('btd,de->bte', attn_ctx, w_out, preferred_element_type=jnp.float32) + b_out.astype(jnp.float32)

        h_mlp, x_norm2, inv_std2 = layer_norm(x_rows, ln2_gain, ln2_bias)
        h_mlp = h_mlp.astype(jnp.bfloat16)
        up_proj = jnp.einsum('btd,df->btf', h_mlp, w_up, preferred_element_type=jnp.float32) + b_up.astype(jnp.float32)
        gelu_out, gelu_back = jax.vjp(exact_gelu, up_proj)
        gelu_bf = gelu_out.astype(jnp.bfloat16)
        mlp_proj = jnp.einsum('btf,fd->btd', gelu_bf, w_down, preferred_element_type=jnp.float32) + b_down.astype(jnp.float32)
        y_rows = (x_rows + attn_proj + mlp_proj).astype(jnp.bfloat16)

        dy_bf = dy_blk.astype(jnp.bfloat16)
        dy_sum = jnp.sum(dy_blk, axis=(0, 1))
        d_w_down = jnp.einsum('btf,btd->fd', gelu_bf, dy_bf, preferred_element_type=jnp.float32)
        d_gelu = jnp.einsum('btd,fd->btf', dy_bf, w_down, preferred_element_type=jnp.float32)
        d_up = gelu_back(d_gelu)[0]
        d_b_up = jnp.sum(d_up, axis=(0, 1))
        d_up_bf = d_up.astype(jnp.bfloat16)
        d_w_up = jnp.einsum('btd,btf->df', h_mlp, d_up_bf, preferred_element_type=jnp.float32)
        d_h_mlp = jnp.einsum('btf,df->btd', d_up_bf, w_up, preferred_element_type=jnp.float32)

        d_w_out = jnp.einsum('btd,bte->de', attn_ctx, dy_bf, preferred_element_type=jnp.float32)
        d_ctx = jnp.einsum('bte,de->btd', dy_bf, w_out, preferred_element_type=jnp.float32).reshape(batch_size, row_count, head_count, head_dim)
        row_delta = jnp.swapaxes(jnp.sum(d_ctx * attn_norm, axis=-1), 1, 2)
        d_ctx_bf = d_ctx.astype(jnp.bfloat16)
        dq_own, dk_own, dv_own = block_grads(q_rows, k_own, v_own, d_ctx_bf, log_sum, row_delta, qk_scale, diag_mask)

        def bwd_step(step_idx, carry):
            k_cur, v_cur, dk_cur, dv_cur, dq_acc = carry
            k_cur, v_cur, dk_cur, dv_cur = lax.ppermute((k_cur, v_cur, dk_cur, dv_cur), 'cp', shift_perm)

            def add_block(operands):
                dq_in, dk_in, dv_in = operands
                g_q, g_k, g_v = block_grads(q_rows, k_cur, v_cur, d_ctx_bf, log_sum, row_delta, qk_scale, None)
                return dq_in + g_q, dk_in + g_k, dv_in + g_v

            dq_acc, dk_cur, dv_cur = lax.cond(step_idx <= my_idx, add_block, lambda operands: operands, (dq_acc, dk_cur, dv_cur))
            return k_cur, v_cur, dk_cur, dv_cur, dq_acc

        loop_out = lax.fori_loop(1, cp_size, bwd_step, (k_own, v_own, dk_own, dv_own, dq_own))
        d_q = loop_out[4]
        d_k, d_v = lax.ppermute((loop_out[2], loop_out[3]), 'cp', shift_perm)

        d_q_raw = apply_rotary(d_q, cos_t, -sin_t)
        d_k_raw = apply_rotary(d_k, cos_t, -sin_t)
        d_qkv = jnp.stack([d_q_raw, d_k_raw, d_v], axis=3)
        d_b_qkv = jnp.sum(d_qkv, axis=(0, 1))
        d_qkv_bf = d_qkv.astype(jnp.bfloat16)
        d_w_qkv = jnp.einsum('btd,bthce->dhce', h_attn, d_qkv_bf, preferred_element_type=jnp.float32)
        d_h_attn = jnp.einsum('bthce,dhce->btd', d_qkv_bf, w_qkv, preferred_element_type=jnp.float32)

        dx_attn, d_ln1_gain, d_ln1_bias = norm_backward(d_h_attn, x_norm1, inv_std1, ln1_gain)
        dx_mlp, d_ln2_gain, d_ln2_bias = norm_backward(d_h_mlp, x_norm2, inv_std2, ln2_gain)
        dx_rows = dy_blk + dx_attn + dx_mlp

        summed = lax.psum((d_ln1_gain, d_ln1_bias, d_ln2_gain, d_ln2_bias, d_w_qkv, d_b_qkv, d_w_out, dy_sum, d_w_up, d_b_up, d_w_down), 'cp')
        return (y_rows, dx_rows) + tuple(summed) + (summed[7],)

    return jax.shard_map(local_layer, mesh=mesh, in_specs=in_specs, out_specs=out_specs, check_vma=False)
```

profile of v0, /device:TPU:0, one launch (start us, length us, event | category | flops | bytes accessed | tf_op | source)
XLA Modules:
  0.0 3873.8 jit_solution(8409357627063372983)
XLA Ops:
  69.7 45.8 %fusion.17 = (f32[2,16,1024]{2,1,0:T(8,128)S(1)}, f32[2,16,1024,1024]{2,3,1,0:T(8,128)}) fusion(pred[1024,1024]{0,1:T(8,128)(4,1)} %iota_compare_fusion, bf16[2,1024,16,48]{1,3,2,0:T(8,128)(2,1)S(1)} %slice.99, bf16[2,1024,16,8]{1,3,2,0:T(8,128)(2,1)} %copy-done.13, bf16[2,1024,16,8]{1,3,2,0:T(8,128)(2,1)} %copy-done.14, ...), kind=kOutput, calls=%fused_computation.25 | convolution fusion | flops 4420763648 | bytes 143785984 | tf_op jit(solution)/shard_map/bqhe,bkhe->bhqk/dot_general | solution.py:46
  157.1 49.7 %bitcast_add_fusion.4 = f32[2,1024,16,64]{1,3,2,0:T(8,128)} fusion(f32[2,1024,16]{1,2,0:T(8,128)S(1)} %get-tuple-element.505, f32[2,16,1024,1024]{2,3,1,0:T(8,128)} %get-tuple-element.515, f32[2,16,1024]{2,1,0:T(8,128)S(1)} %broadcast_maximum_fusion, pred[1024,1024]{0,1:T(8,128)(4,1)} %iota_compare_fusion, f32[2,1024,16,3,64]{1,4,3,2,0:T(8,128)} %broadcast_add_fusion), kind=kOutput, calls=%fused_computation.104 | convolution fusion | flops 4431282176 | bytes 148111360 | tf_op jit(solution)/shard_map/bhqk,bkhe->bqhe/dot_general | solution.py:59
  223.2 580.2 %while.42 = (s32[]{:T(128)}, bf16[2,1024,16,64]{1,3,2,0:T(8,128)(2,1)}, bf16[2,1024,16,64]{1,3,2,0:T(8,128)(2,1)}, f32[2,16,1024]{2,1,0:T(8,128)S(1)}, f32[2,16,...) while((s32[]{:T(128)}, ...), condition=%wide.region_9.10_spmd, body=%wide.region_4.9_spmd.sunk | while | flops 8862662656 | bytes 484442368 | solution.py:109
  227.1 45.5 %collective-permute-done = bf16[2,1024,16,64]{1,3,2,0:T(8,128)(2,1)} collective-permute-done((bf16[2,1024,16,64]{1,3,2,0:T(8,128)(2,1)}, bf16[2,1024,16,64]{1,3,2,0:T(8,128)(2,1)}, u32[]{:S(2)}, u32[]{:S(2)}) %collective-permute-start) | collective-permute-done | bytes 4194336 | tf_op jit(solution)/shard_map/while/body/eval_jaxpr/ppermute | solution.py:105
  272.6 44.9 %collective-permute-done.1 = bf16[2,1024,16,64]{1,3,2,0:T(8,128)(2,1)} collective-permute-done((bf16[2,1024,16,64]{1,3,2,0:T(8,128)(2,1)}, bf16[2,1024,16,64]{1,3,2,0:T(8,128)(2,1)}, u32[]{:S(2)}, u32[]{:S(2)}) %collective-permute-start.1) | collective-permute-done | bytes 4194336 | tf_op jit(solution)/shard_map/while/body/eval_jaxpr/ppermute | solution.py:105
  327.4 137.7 %collective-permute-start = (bf16[2,1024,16,64]{1,3,2,0:T(8,128)(2,1)}, bf16[2,1024,16,64]{1,3,2,0:T(8,128)(2,1)}, u32[]{:S(2)}, u32[]{:S(2)}) collective-permute-start(bf16[2,1024,16,64]{1,3,2,0:T(8,128)(2,1)} %get-tuple-element.678), channel_id=1, source_target_pairs={{0,1},{1,2},{2,3},{3,0},{4,5},{5,6},{6,7},{7,4}} | collective-permute-start | bytes 12582920 | tf_op jit(solution)/shard_map/while/body/eval_jaxpr/ppermute | solution.py:105
  510.6 44.9 %collective-permute-done.1 = bf16[2,1024,16,64]{1,3,2,0:T(8,128)(2,1)} collective-permute-done((bf16[2,1024,16,64]{1,3,2,0:T(8,128)(2,1)}, bf16[2,1024,16,64]{1,3,2,0:T(8,128)(2,1)}, u32[]{:S(2)}, u32[]{:S(2)}) %collective-permute-start.1) | collective-permute-done | bytes 4194336 | tf_op jit(solution)/shard_map/while/body/eval_jaxpr/ppermute | solution.py:105
  567.8 140.3 %collective-permute-start.1 = (bf16[2,1024,16,64]{1,3,2,0:T(8,128)(2,1)}, bf16[2,1024,16,64]{1,3,2,0:T(8,128)(2,1)}, u32[]{:S(2)}, u32[]{:S(2)}) collective-permute-start(bf16[2,1024,16,64]{1,3,2,0:T(8,128)(2,1)} %get-tuple-element.679), channel_id=1, source_target_pairs={{0,1},{1,2},{2,3},{3,0},{4,5},{5,6},{6,7},{7,4}} | collective-permute-start | bytes 12582920 | tf_op jit(solution)/shard_map/while/body/eval_jaxpr/ppermute | solution.py:105
  813.9 53.5 %fusion.89 = f32[2,1024,16,64]{1,3,2,0:T(8,128)} fusion(bf16[2,1024,16,64]{1,3,2,0:T(8,128)(2,1)} %bitcast.135, f32[2,16,1024,1024]{2,3,1,0:T(8,128)} %get-tuple-element.515, f32[2,16,1024]{2,1,0:T(8,128)S(1)} %log_add_fusion, pred[1024,1024]{0,1:T(8,128)(4,1)} %iota_compare_fusion), kind=kOutput, calls=%fused_computation.125 | convolution fusion | flops 4429185024 | bytes 147980288 | tf_op jit(solution)/shard_map/bhqk,bqhe->bkhe/dot_general | solution.py:67
  867.3 82.6 %multiply_convert_fusion.1 = bf16[2,16,1024,1024]{2,3,1,0:T(8,128)(2,1)} fusion(f32[2,16,1024,1024]{2,3,1,0:T(8,128)} %get-tuple-element.515, f32[2,16,1024]{2,1,0:T(8,128)S(1)} %bitcast.145, f32[2,16,1024]{2,1,0:T(8,128)S(1)} %log_add_fusion, pred[1024,1024]{0,1:T(8,128)(4,1)S(1)} %copy-done.15, bf16[2,1024,16,64]{1,3,2,0:T(8,128)(2,1)} %bitcast.136, ...), kind=kOutput, calls=%fused_computation.18 | convolution fusion | flops 4529848320 | bytes 211025920 | tf_op jit(solution)/shard_map/bqhe,bkhe->bhqk/dot_general | solution.py:68
  1010.4 1493.1 %while.43 = (s32[]{:T(128)}, bf16[2,1024,16,64]{1,3,2,0:T(8,128)(2,1)}, bf16[2,1024,16,64]{1,3,2,0:T(8,128)(2,1)}, f32[2,1024,16,64]{1,3,2,0:T(8,128)}, f32[2,10...) while((s32[]{:T(128)}, ...), condition=%wide.region_14.15_spmd, body=%wide.region_11.14_spmd.sunk | while | flops 21783117824 | bytes 851837312 | solution.py:151
  1018.3 130.2 %collective-permute-start.2 = (bf16[2,1024,16,64]{1,3,2,0:T(8,128)(2,1)}, bf16[2,1024,16,64]{1,3,2,0:T(8,128)(2,1)}, u32[]{:S(2)}, u32[]{:S(2)}) collective-permute-start(bf16[2,1024,16,64]{1,3,2,0:T(8,128)(2,1)} %get-tuple-element.708), channel_id=1, source_target_pairs={{0,1},{1,2},{2,3},{3,0},{4,5},{5,6},{6,7},{7,4}} | collective-permute-start | bytes 12582920 | tf_op jit(solution)/shard_map/while/body/eval_jaxpr/ppermute | solution.py:141
  1148.5 225.4 %collective-permute-done.2 = bf16[2,1024,16,64]{1,3,2,0:T(8,128)(2,1)} collective-permute-done((bf16[2,1024,16,64]{1,3,2,0:T(8,128)(2,1)}, bf16[2,1024,16,64]{1,3,2,0:T(8,128)(2,1)}, u32[]{:S(2)}, u32[]{:S(2)}) %collective-permute-start.2) | collective-permute-done | bytes 4194336 | tf_op jit(solution)/shard_map/while/body/eval_jaxpr/ppermute | solution.py:141
  1440.6 149.3 %collective-permute-start.4 = (f32[2,1024,16,64]{1,3,2,0:T(8,128)}, f32[2,1024,16,64]{1,3,2,0:T(8,128)}, u32[]{:S(2)}, u32[]{:S(2)}) collective-permute-start(f32[2,1024,16,64]{1,3,2,0:T(8,128)} %get-tuple-element.710), channel_id=1, source_target_pairs={{0,1},{1,2},{2,3},{3,0},{4,5},{5,6},{6,7},{7,4}} | collective-permute-start | bytes 25165832 | tf_op jit(solution)/shard_map/while/body/eval_jaxpr/ppermute | solution.py:141
  1592.4 87.4 %collective-permute-start.2 = (bf16[2,1024,16,64]{1,3,2,0:T(8,128)(2,1)}, bf16[2,1024,16,64]{1,3,2,0:T(8,128)(2,1)}, u32[]{:S(2)}, u32[]{:S(2)}) collective-permute-start(bf16[2,1024,16,64]{1,3,2,0:T(8,128)(2,1)} %get-tuple-element.708), channel_id=1, source_target_pairs={{0,1},{1,2},{2,3},{3,0},{4,5},{5,6},{6,7},{7,4}} | collective-permute-start | bytes 12582920 | tf_op jit(solution)/shard_map/while/body/eval_jaxpr/ppermute | solution.py:141
  1679.8 225.4 %collective-permute-done.2 = bf16[2,1024,16,64]{1,3,2,0:T(8,128)(2,1)} collective-permute-done((bf16[2,1024,16,64]{1,3,2,0:T(8,128)(2,1)}, bf16[2,1024,16,64]{1,3,2,0:T(8,128)(2,1)}, u32[]{:S(2)}, u32[]{:S(2)}) %collective-permute-start.2) | collective-permute-done | bytes 4194336 | tf_op jit(solution)/shard_map/while/body/eval_jaxpr/ppermute | solution.py:141
  1972.0 154.3 %collective-permute-start.5 = (f32[2,1024,16,64]{1,3,2,0:T(8,128)}, f32[2,1024,16,64]{1,3,2,0:T(8,128)}, u32[]{:S(2)}, u32[]{:S(2)}) collective-permute-start(f32[2,1024,16,64]{1,3,2,0:T(8,128)} %get-tuple-element.711), channel_id=1, source_target_pairs={{0,1},{1,2},{2,3},{3,0},{4,5},{5,6},{6,7},{7,4}} | collective-permute-start | bytes 25165832 | tf_op jit(solution)/shard_map/while/body/eval_jaxpr/ppermute | solution.py:141
  2126.2 84.9 %collective-permute-start.2 = (bf16[2,1024,16,64]{1,3,2,0:T(8,128)(2,1)}, bf16[2,1024,16,64]{1,3,2,0:T(8,128)(2,1)}, u32[]{:S(2)}, u32[]{:S(2)}) collective-permute-start(bf16[2,1024,16,64]{1,3,2,0:T(8,128)(2,1)} %get-tuple-element.708), channel_id=1, source_target_pairs={{0,1},{1,2},{2,3},{3,0},{4,5},{5,6},{6,7},{7,4}} | collective-permute-start | bytes 12582920 | tf_op jit(solution)/shard_map/while/body/eval_jaxpr/ppermute | solution.py:141
  2211.2 225.4 %collective-permute-done.2 = bf16[2,1024,16,64]{1,3,2,0:T(8,128)(2,1)} collective-permute-done((bf16[2,1024,16,64]{1,3,2,0:T(8,128)(2,1)}, bf16[2,1024,16,64]{1,3,2,0:T(8,128)(2,1)}, u32[]{:S(2)}, u32[]{:S(2)}) %collective-permute-start.2) | collective-permute-done | bytes 4194336 | tf_op jit(solution)/shard_map/while/body/eval_jaxpr/ppermute | solution.py:141
  2548.5 80.9 %multiply_convert_fusion.2 = (bf16[2,1024,4096]{2,1,0:T(8,128)(2,1)}, f32[2,1024,4096]{2,1,0:T(8,128)}) fusion(f32[2,1024,4096]{2,1,0:T(8,128)} %get-tuple-element.517, f32[4096]{0:T(1024)S(1)} %convert_element_type.96, u8[1024,4096]{1,0:T(8,128)(4,1)} %get-tuple-element.423, u8[1024,4096]{1,0:T(8,128)(4,1)} %get-tuple-element.422), kind=kLoop, calls=%fused_computation.38 | loop fusion | flops 595591168 | bytes 92291072 | tf_op jit(solution)/shard_map/convert_element_type | solution.py:119
  2728.7 104.6 %collective-permute-done.6 = f32[2,1024,16,64]{1,3,2,0:T(8,128)} collective-permute-done((f32[2,1024,16,64]{1,3,2,0:T(8,128)}, f32[2,1024,16,64]{1,3,2,0:T(8,128)}, u32[]{:S(2)}, u32[]{:S(2)}) %collective-permute-start.6) | collective-permute-done | bytes 8388640 | tf_op jit(solution)/shard_map/ppermute | solution.py:153
  2847.0 76.2 %collective-permute-done.7 = f32[2,1024,16,64]{1,3,2,0:T(8,128)} collective-permute-done((f32[2,1024,16,64]{1,3,2,0:T(8,128)}, f32[2,1024,16,64]{1,3,2,0:T(8,128)}, u32[]{:S(2)}, u32[]{:S(2)}) %collective-permute-start.7) | collective-permute-done | bytes 8388640 | tf_op jit(solution)/shard_map/ppermute | solution.py:153
  3035.7 71.9 %all-reduce = (f32[1024]{0:T(1024)}, f32[1024]{0:T(1024)}, f32[1024]{0:T(1024)}, f32[1024]{0:T(1024)}, f32[16,3,64]{2,0,1:T(8,128)}, /*index=5*/f32[1024]{0:T(1024)S(1)}, f32[4096]{0:T(1024)}) all-reduce(f32[1024]{0:T(1024)S(1)} %get-tuple-element.426, f32[1024]{0:T(1024)S(1)} %get-tuple-element.431, ...), channel_id=1, replica_groups=mesh['dp'=2,'cp'=4] {'cp'}, use_global_device_ids=true, to_apply=%region_20.21 | all-reduce | flops 12288 | bytes 98304 | tf_op jit(solution)/shard_map/psum | solution.py:167
  3122.2 707.1 %all-reduce.4.cloned.1.call-done = (f32[1024,16,3,64]{0,3,2,1:T(8,128)}, f32[1024,1024]{1,0:T(8,128)}, f32[1024,4096]{1,0:T(8,128)}, f32[4096,1024]{1,0:T(8,128)}) async-done(((f32[1024,16,3,64]{0,3,2,1:T(8,128)}, f32[1024,1024]{1,0:T(8,128)}, f32[1024,4096]{1,0:T(8,128)}, f32[4096,1024]{1,0:T(8,128)}), (f32[1024,16,3,64]{0,3,2,1:T(8,128)}, f32[1024,1024]{1,0:T(8,128)}, f32[1024,4096]{1,0:T(8,128)}, ...) | async-done | bytes 50331664 | tf_op jit(solution)/shard_map/psum | solution.py:167
  (196 shorter events, 890.0 us)
Async XLA Ops:
  7.2 3822.1 %all-reduce.4.cloned.1.call-start = ((), (), s32[]{:S(2)}) async-start(), calls=%async_computation | async-start | bytes 100663296 | tf_op jit(solution)/shard_map/psum | solution.py:167
  223.6 49.0 %collective-permute-start = (bf16[2,1024,16,64]{1,3,2,0:T(8,128)(2,1)}, bf16[2,1024,16,64]{1,3,2,0:T(8,128)(2,1)}, u32[]{:S(2)}, u32[]{:S(2)}) collective-permute-start(bf16[2,1024,16,64]{1,3,2,0:T(8,128)(2,1)} %get-tuple-element.678), channel_id=1, source_target_pairs={{0,1},{1,2},{2,3},{3,0},{4,5},{5,6},{6,7},{7,4}} | collective-permute-start | bytes 12582920 | tf_op jit(solution)/shard_map/while/body/eval_jaxpr/ppermute | solution.py:105
  224.5 93.1 %collective-permute-start.1 = (bf16[2,1024,16,64]{1,3,2,0:T(8,128)(2,1)}, bf16[2,1024,16,64]{1,3,2,0:T(8,128)(2,1)}, u32[]{:S(2)}, u32[]{:S(2)}) collective-permute-start(bf16[2,1024,16,64]{1,3,2,0:T(8,128)(2,1)} %get-tuple-element.679), channel_id=1, source_target_pairs={{0,1},{1,2},{2,3},{3,0},{4,5},{5,6},{6,7},{7,4}} | collective-permute-start | bytes 12582920 | tf_op jit(solution)/shard_map/while/body/eval_jaxpr/ppermute | solution.py:105
  327.4 183.2 %collective-permute-start = (bf16[2,1024,16,64]{1,3,2,0:T(8,128)(2,1)}, bf16[2,1024,16,64]{1,3,2,0:T(8,128)(2,1)}, u32[]{:S(2)}, u32[]{:S(2)}) collective-permute-start(bf16[2,1024,16,64]{1,3,2,0:T(8,128)(2,1)} %get-tuple-element.678), channel_id=1, source_target_pairs={{0,1},{1,2},{2,3},{3,0},{4,5},{5,6},{6,7},{7,4}} | collective-permute-start | bytes 12582920 | tf_op jit(solution)/shard_map/while/body/eval_jaxpr/ppermute | solution.py:105
  465.1 90.5 %collective-permute-start.1 = (bf16[2,1024,16,64]{1,3,2,0:T(8,128)(2,1)}, bf16[2,1024,16,64]{1,3,2,0:T(8,128)(2,1)}, u32[]{:S(2)}, u32[]{:S(2)}) collective-permute-start(bf16[2,1024,16,64]{1,3,2,0:T(8,128)(2,1)} %get-tuple-element.679), channel_id=1, source_target_pairs={{0,1},{1,2},{2,3},{3,0},{4,5},{5,6},{6,7},{7,4}} | collective-permute-start | bytes 12582920 | tf_op jit(solution)/shard_map/while/body/eval_jaxpr/ppermute | solution.py:105
  565.4 183.2 %collective-permute-start = (bf16[2,1024,16,64]{1,3,2,0:T(8,128)(2,1)}, bf16[2,1024,16,64]{1,3,2,0:T(8,128)(2,1)}, u32[]{:S(2)}, u32[]{:S(2)}) collective-permute-start(bf16[2,1024,16,64]{1,3,2,0:T(8,128)(2,1)} %get-tuple-element.678), channel_id=1, source_target_pairs={{0,1},{1,2},{2,3},{3,0},{4,5},{5,6},{6,7},{7,4}} | collective-permute-start | bytes 12582920 | tf_op jit(solution)/shard_map/while/body/eval_jaxpr/ppermute | solution.py:105
  567.8 225.8 %collective-permute-start.1 = (bf16[2,1024,16,64]{1,3,2,0:T(8,128)(2,1)}, bf16[2,1024,16,64]{1,3,2,0:T(8,128)(2,1)}, u32[]{:S(2)}, u32[]{:S(2)}) collective-permute-start(bf16[2,1024,16,64]{1,3,2,0:T(8,128)(2,1)} %get-tuple-element.679), channel_id=1, source_target_pairs={{0,1},{1,2},{2,3},{3,0},{4,5},{5,6},{6,7},{7,4}} | collective-permute-start | bytes 12582920 | tf_op jit(solution)/shard_map/while/body/eval_jaxpr/ppermute | solution.py:105
  1010.4 1493.2 %copy-start.24 = (f32[2,1024]{1,0:T(2,128)S(1)}, f32[2,1024]{1,0:T(2,128)}, u32[]{:S(2)}) copy-start(f32[2,1024]{1,0:T(2,128)} %copy-done.23) | copy-start | bytes 24580
  1010.4 1493.2 %copy-start.31 = (f32[1024]{0:T(1024)S(1)}, f32[1024]{0:T(1024)}, u32[]{:S(2)}) copy-start(f32[1024]{0:T(1024)} %param.26) | copy-start | bytes 12292
  1010.4 1493.2 %copy-start.36 = (f32[1024]{0:T(1024)S(1)}, f32[1024]{0:T(1024)}, u32[]{:S(2)}) copy-start(f32[1024]{0:T(1024)} %param.27) | copy-start | bytes 12292
  1010.8 412.9 %collective-permute-start.4 = (f32[2,1024,16,64]{1,3,2,0:T(8,128)}, f32[2,1024,16,64]{1,3,2,0:T(8,128)}, u32[]{:S(2)}, u32[]{:S(2)}) collective-permute-start(f32[2,1024,16,64]{1,3,2,0:T(8,128)} %get-tuple-element.710), channel_id=1, source_target_pairs={{0,1},{1,2},{2,3},{3,0},{4,5},{5,6},{6,7},{7,4}} | collective-permute-start | bytes 25165832 | tf_op jit(solution)/shard_map/while/body/eval_jaxpr/ppermute | solution.py:141
  1015.8 408.0 %collective-permute-start.5 = (f32[2,1024,16,64]{1,3,2,0:T(8,128)}, f32[2,1024,16,64]{1,3,2,0:T(8,128)}, u32[]{:S(2)}, u32[]{:S(2)}) collective-permute-start(f32[2,1024,16,64]{1,3,2,0:T(8,128)} %get-tuple-element.711), channel_id=1, source_target_pairs={{0,1},{1,2},{2,3},{3,0},{4,5},{5,6},{6,7},{7,4}} | collective-permute-start | bytes 25165832 | tf_op jit(solution)/shard_map/while/body/eval_jaxpr/ppermute | solution.py:141
  1018.3 355.6 %collective-permute-start.2 = (bf16[2,1024,16,64]{1,3,2,0:T(8,128)(2,1)}, bf16[2,1024,16,64]{1,3,2,0:T(8,128)(2,1)}, u32[]{:S(2)}, u32[]{:S(2)}) collective-permute-start(bf16[2,1024,16,64]{1,3,2,0:T(8,128)(2,1)} %get-tuple-element.708), channel_id=1, source_target_pairs={{0,1},{1,2},{2,3},{3,0},{4,5},{5,6},{6,7},{7,4}} | collective-permute-start | bytes 12582920 | tf_op jit(solution)/shard_map/while/body/eval_jaxpr/ppermute | solution.py:141
  1148.4 270.4 %collective-permute-start.3 = (bf16[2,1024,16,64]{1,3,2,0:T(8,128)(2,1)}, bf16[2,1024,16,64]{1,3,2,0:T(8,128)(2,1)}, u32[]{:S(2)}, u32[]{:S(2)}) collective-permute-start(bf16[2,1024,16,64]{1,3,2,0:T(8,128)(2,1)} %get-tuple-element.709), channel_id=1, source_target_pairs={{0,1},{1,2},{2,3},{3,0},{4,5},{5,6},{6,7},{7,4}} | collective-permute-start | bytes 12582920 | tf_op jit(solution)/shard_map/while/body/eval_jaxpr/ppermute | solution.py:141
  1440.6 514.5 %collective-permute-start.4 = (f32[2,1024,16,64]{1,3,2,0:T(8,128)}, f32[2,1024,16,64]{1,3,2,0:T(8,128)}, u32[]{:S(2)}, u32[]{:S(2)}) collective-permute-start(f32[2,1024,16,64]{1,3,2,0:T(8,128)} %get-tuple-element.710), channel_id=1, source_target_pairs={{0,1},{1,2},{2,3},{3,0},{4,5},{5,6},{6,7},{7,4}} | collective-permute-start | bytes 25165832 | tf_op jit(solution)/shard_map/while/body/eval_jaxpr/ppermute | solution.py:141
  1589.9 365.2 %collective-permute-start.5 = (f32[2,1024,16,64]{1,3,2,0:T(8,128)}, f32[2,1024,16,64]{1,3,2,0:T(8,128)}, u32[]{:S(2)}, u32[]{:S(2)}) collective-permute-start(f32[2,1024,16,64]{1,3,2,0:T(8,128)} %get-tuple-element.711), channel_id=1, source_target_pairs={{0,1},{1,2},{2,3},{3,0},{4,5},{5,6},{6,7},{7,4}} | collective-permute-start | bytes 25165832 | tf_op jit(solution)/shard_map/while/body/eval_jaxpr/ppermute | solution.py:141
  1592.4 312.8 %collective-permute-start.2 = (bf16[2,1024,16,64]{1,3,2,0:T(8,128)(2,1)}, bf16[2,1024,16,64]{1,3,2,0:T(8,128)(2,1)}, u32[]{:S(2)}, u32[]{:S(2)}) collective-permute-start(bf16[2,1024,16,64]{1,3,2,0:T(8,128)(2,1)} %get-tuple-element.708), channel_id=1, source_target_pairs={{0,1},{1,2},{2,3},{3,0},{4,5},{5,6},{6,7},{7,4}} | collective-permute-start | bytes 12582920 | tf_op jit(solution)/shard_map/while/body/eval_jaxpr/ppermute | solution.py:141
  1679.8 270.4 %collective-permute-start.3 = (bf16[2,1024,16,64]{1,3,2,0:T(8,128)(2,1)}, bf16[2,1024,16,64]{1,3,2,0:T(8,128)(2,1)}, u32[]{:S(2)}, u32[]{:S(2)}) collective-permute-start(bf16[2,1024,16,64]{1,3,2,0:T(8,128)(2,1)} %get-tuple-element.709), channel_id=1, source_target_pairs={{0,1},{1,2},{2,3},{3,0},{4,5},{5,6},{6,7},{7,4}} | collective-permute-start | bytes 12582920 | tf_op jit(solution)/shard_map/while/body/eval_jaxpr/ppermute | solution.py:141
  1972.0 514.5 %collective-permute-start.4 = (f32[2,1024,16,64]{1,3,2,0:T(8,128)}, f32[2,1024,16,64]{1,3,2,0:T(8,128)}, u32[]{:S(2)}, u32[]{:S(2)}) collective-permute-start(f32[2,1024,16,64]{1,3,2,0:T(8,128)} %get-tuple-element.710), channel_id=1, source_target_pairs={{0,1},{1,2},{2,3},{3,0},{4,5},{5,6},{6,7},{7,4}} | collective-permute-start | bytes 25165832 | tf_op jit(solution)/shard_map/while/body/eval_jaxpr/ppermute | solution.py:141
  1972.0 514.5 %collective-permute-start.5 = (f32[2,1024,16,64]{1,3,2,0:T(8,128)}, f32[2,1024,16,64]{1,3,2,0:T(8,128)}, u32[]{:S(2)}, u32[]{:S(2)}) collective-permute-start(f32[2,1024,16,64]{1,3,2,0:T(8,128)} %get-tuple-element.711), channel_id=1, source_target_pairs={{0,1},{1,2},{2,3},{3,0},{4,5},{5,6},{6,7},{7,4}} | collective-permute-start | bytes 25165832 | tf_op jit(solution)/shard_map/while/body/eval_jaxpr/ppermute | solution.py:141
  2126.2 310.3 %collective-permute-start.2 = (bf16[2,1024,16,64]{1,3,2,0:T(8,128)(2,1)}, bf16[2,1024,16,64]{1,3,2,0:T(8,128)(2,1)}, u32[]{:S(2)}, u32[]{:S(2)}) collective-permute-start(bf16[2,1024,16,64]{1,3,2,0:T(8,128)(2,1)} %get-tuple-element.708), channel_id=1, source_target_pairs={{0,1},{1,2},{2,3},{3,0},{4,5},{5,6},{6,7},{7,4}} | collective-permute-start | bytes 12582920 | tf_op jit(solution)/shard_map/while/body/eval_jaxpr/ppermute | solution.py:141
  2211.1 270.4 %collective-permute-start.3 = (bf16[2,1024,16,64]{1,3,2,0:T(8,128)(2,1)}, bf16[2,1024,16,64]{1,3,2,0:T(8,128)(2,1)}, u32[]{:S(2)}, u32[]{:S(2)}) collective-permute-start(bf16[2,1024,16,64]{1,3,2,0:T(8,128)(2,1)} %get-tuple-element.709), channel_id=1, source_target_pairs={{0,1},{1,2},{2,3},{3,0},{4,5},{5,6},{6,7},{7,4}} | collective-permute-start | bytes 12582920 | tf_op jit(solution)/shard_map/while/body/eval_jaxpr/ppermute | solution.py:141
  2503.5 329.8 %collective-permute-start.6 = (f32[2,1024,16,64]{1,3,2,0:T(8,128)}, f32[2,1024,16,64]{1,3,2,0:T(8,128)}, u32[]{:S(2)}, u32[]{:S(2)}) collective-permute-start(f32[2,1024,16,64]{1,3,2,0:T(8,128)} %get-tuple-element.420), channel_id=1, source_target_pairs={{0,1},{1,2},{2,3},{3,0},{4,5},{5,6},{6,7},{7,4}} | collective-permute-start | bytes 25165832 | tf_op jit(solution)/shard_map/ppermute | solution.py:153
  2503.5 419.7 %collective-permute-start.7 = (f32[2,1024,16,64]{1,3,2,0:T(8,128)}, f32[2,1024,16,64]{1,3,2,0:T(8,128)}, u32[]{:S(2)}, u32[]{:S(2)}) collective-permute-start(f32[2,1024,16,64]{1,3,2,0:T(8,128)} %get-tuple-element.421), channel_id=1, source_target_pairs={{0,1},{1,2},{2,3},{3,0},{4,5},{5,6},{6,7},{7,4}} | collective-permute-start | bytes 25165832 | tf_op jit(solution)/shard_map/ppermute | solution.py:153
  (41 other events, 5347.6 us)
Sparse Core Ops, SparseCore 0:
  2946.2 883.0 all-reduce.3
where the time goes:
time: 3880 us; the launch traced here: 3870 us
  waiting for transfers between devices  1950 us (50%)
  starting transfers between devices  903 us (23%)
  matrix products  567 us (15%)
  local copies, waits for them, and re-layouts  190 us (5%)
  other arithmetic  179 us (5%)
  blocking collectives  71.9 us (2%)
    ppermute x12, waiting for transfers between devices, bwd_step(): lax.ppermute((k_cur, v_cur, dk_cur, dv_cur), 'cp', shift_perm)  796 us
    psum x1, waiting for transfers between devices, local_layer(): lax.psum((d_ln1_gain, d_ln1_bias, d_ln2_gain, d_ln2_bias, d_w_qkv, d_b_qk...  707 us
    ppermute x12, starting transfers between devices, bwd_step(): lax.ppermute((k_cur, v_cur, dk_cur, dv_cur), 'cp', shift_perm)  616 us
    ppermute x6, starting transfers between devices, fwd_step(): k_cur, v_cur = lax.ppermute((k_cur, v_cur), 'cp', shift_perm)  286 us
    ppermute x6, waiting for transfers between devices, fwd_step(): k_cur, v_cur = lax.ppermute((k_cur, v_cur), 'cp', shift_perm)  264 us
    ppermute x2, waiting for transfers between devices, local_layer(): d_k, d_v = lax.ppermute((loop_out[2], loop_out[3]), 'cp', shift_perm)  181 us
    while x18, local copies, waits for them, and re-layouts  110 us
    dot_general x1, matrix products, block_grads(): jnp.einsum('bqhe,bkhe->bhqk', d_ctx_bf, v_blk, preferred_element_type=jnp...  82.6 us
  transfers between devices with their start and end apart: 21, of which 15 were waited for; matrix products, arithmetic and copies ran while one was open for 10% of the time, Pallas kernels for 0%

commit v1 on v0

v1 whole, which is shorter than its diff:
```python
import jax
import jax.numpy as jnp
from jax import lax
from jax.experimental import pallas as pl
from jax.experimental.pallas import tpu as pltpu
from jax.sharding import PartitionSpec as P

EPS = 1e-5
ROPE_BASE = 10000.0
NEG_BIG = -1e30
LOG2E = 1.4426950408889634
HD = 64
BLK = 1024
SUB = 256
BK = 512


def nn_dot(lhs, rhs):
    return lax.dot_general(lhs, rhs, (((1,), (0,)), ((), ())), preferred_element_type=jnp.float32)


def nt_dot(lhs, rhs):
    return lax.dot_general(lhs, rhs, (((1,), (1,)), ((), ())), preferred_element_type=jnp.float32)


def turn(rows, cos_t, sin_t):
    lo, hi = rows[0:8], rows[8:16]
    return jnp.concatenate([lo * cos_t - hi * sin_t, hi * cos_t + lo * sin_t, rows[16:]], axis=0)


def fwd_kernel(n_blk, coef, me_ref, cos_ref, sin_ref, bias_ref, *refs):
    slots = refs[:n_blk]
    qkv_ref, out_ref, lse_ref = refs[n_blk:n_blk + 3]
    ctx_refs = refs[n_blk + 3:2 * n_blk + 3]
    k_nat, s_a, s_b = refs[2 * n_blk + 3:]
    me = me_ref[0]
    bias = bias_ref[...]
    for s in range(n_blk):
        cols = pl.ds(pl.multiple_of(jnp.bitwise_xor(me, s) * BLK, BLK), BLK)
        cos_t, sin_t = cos_ref[:, cols], sin_ref[:, cols]
        rows = slots[s][...] + bias
        q_t = turn(rows[0:HD], cos_t, sin_t)
        k_t = turn(rows[HD:2 * HD], cos_t, sin_t)
        qkv_ref[0, 0:HD, cols] = q_t.astype(jnp.bfloat16)
        qkv_ref[0, HD:2 * HD, cols] = k_t.astype(jnp.bfloat16)
        qkv_ref[0, 2 * HD:3 * HD, cols] = rows[2 * HD:].astype(jnp.bfloat16)
        k_nat[cols, :] = k_t.T.astype(jnp.bfloat16)

    n_sub = BLK // SUB

    def q_cols(q_idx, sub):
        return pl.ds(pl.multiple_of(q_idx * BLK + sub * SUB, SUB), SUB)

    def make(q_idx, k_start, sub, k_len, buf):
        scores = nn_dot(k_nat[pl.ds(pl.multiple_of(k_start, SUB), k_len), :], qkv_ref[0, 0:HD, q_cols(q_idx, sub)])
        return scores

    def put(q_idx, k_start, sub, buf):
        scores = make(q_idx, k_start, sub, BK, buf)
        buf[:, sub * SUB:(sub + 1) * SUB] = scores
        return jnp.max(scores, axis=0, keepdims=True)

    def take(state, top, k_start, scores):
        old_max, tot, acc = state
        new_max = jnp.maximum(old_max, top)
        probs = jnp.exp2((scores - new_max) * coef)
        fade = jnp.exp2((old_max - new_max) * coef)
        tot = tot * fade + jnp.sum(probs, axis=0, keepdims=True)
        v_t = qkv_ref[0, 2 * HD:3 * HD, pl.ds(pl.multiple_of(k_start, SUB), scores.shape[0])]
        acc = acc * fade + nn_dot(v_t, probs.astype(jnp.bfloat16))
        return new_max, tot, acc

    def one_q(q_idx, _):
        base = q_idx * BLK
        tops = tuple(put(q_idx, 0, c, s_a) for c in range(n_sub))
        start = tuple((jnp.full((1, SUB), NEG_BIG, jnp.float32), jnp.zeros((1, SUB), jnp.float32), jnp.zeros((HD, SUB), jnp.float32)) for _ in range(n_sub))

        def pair(j, carry):
            states, tops_a = carry
            k0 = j * (2 * BK)
            tops_b, mid = [], []
            for c in range(n_sub):
                tops_b.append(put(q_idx, k0 + BK, c, s_b))
                mid.append(take(states[c], tops_a[c], k0, s_a[:, c * SUB:(c + 1) * SUB]))
            tops_n, fin = [], []
            for c in range(n_sub):
                tops_n.append(put(q_idx, k0 + 2 * BK, c, s_a))
                fin.append(take(mid[c], tops_b[c], k0 + BK, s_b[:, c * SUB:(c + 1) * SUB]))
            return tuple(fin), tuple(tops_n)

        states, tops = lax.fori_loop(0, q_idx, pair, (start, tops))
        states = list(states)
        tri = lax.broadcasted_iota(jnp.int32, (SUB, SUB), 0) <= lax.broadcasted_iota(jnp.int32, (SUB, SUB), 1)

        def masked(scores):
            return jnp.where(tri, scores, NEG_BIG)

        half = n_sub // 2
        for c in range(n_sub):
            if c < half:
                for r in range(c):
                    part = s_a[r * SUB:(r + 1) * SUB, c * SUB:(c + 1) * SUB]
                    states[c] = take(states[c], jnp.max(part, axis=0, keepdims=True), base + r * SUB, part)
                part = masked(s_a[c * SUB:(c + 1) * SUB, c * SUB:(c + 1) * SUB])
                states[c] = take(states[c], jnp.max(part, axis=0, keepdims=True), base + c * SUB, part)
            else:
                states[c] = take(states[c], tops[c], base, s_a[:, c * SUB:(c + 1) * SUB])
                for r in range(half, c + 1):
                    part = make(q_idx, base + r * SUB, c, SUB, None)
                    if r == c:
                        part = masked(part)
                    states[c] = take(states[c], jnp.max(part, axis=0, keepdims=True), base + r * SUB, part)
        for c in range(n_sub):
            top, tot, acc = states[c]
            outs = acc / tot
            out_ref[0, :, q_cols(q_idx, c)] = outs
            lse_ref[0, :, q_cols(q_idx, c)] = top * coef + jnp.log2(tot)
        return 0

    lax.fori_loop(0, n_blk, one_q, 0)
    for s in range(n_blk):
        cols = pl.ds(pl.multiple_of(jnp.bitwise_xor(me, s) * BLK, BLK), BLK)
        ctx_refs[s][...] = out_ref[0, :, cols].astype(jnp.bfloat16)


def attn_fwd(me, cos_t, sin_t, bias_col, slots, coef):
    n_blk = len(slots)
    rows, toks = slots[0].shape
    heads, batch, seq = rows // (3 * HD), toks // BLK, n_blk * BLK
    n_pair = heads * batch
    full = lambda h, b, me: (0, 0)
    hb = lambda h, b, me: (h, b)
    one = lambda h, b, me: (h * batch + b, 0, 0)
    return pl.pallas_call(
        lambda *refs: fwd_kernel(n_blk, coef, *refs),
        grid_spec=pltpu.PrefetchScalarGridSpec(
            num_scalar_prefetch=1, grid=(heads, batch),
            in_specs=[pl.BlockSpec((8, seq), full), pl.BlockSpec((8, seq), full), pl.BlockSpec((3 * HD, 1), lambda h, b, me: (h, 0))] + [pl.BlockSpec((3 * HD, BLK), hb)] * n_blk,
            out_specs=[pl.BlockSpec((1, 3 * HD, seq), one), pl.BlockSpec((1, HD, seq), one), pl.BlockSpec((1, 1, seq), one)] + [pl.BlockSpec((HD, BLK), hb)] * n_blk,
            scratch_shapes=[pltpu.VMEM((seq, HD), jnp.bfloat16), pltpu.VMEM((BK, BLK), jnp.float32), pltpu.VMEM((BK, BLK), jnp.float32)]),
        out_shape=[jax.ShapeDtypeStruct((n_pair, 3 * HD, seq), jnp.bfloat16), jax.ShapeDtypeStruct((n_pair, HD, seq), jnp.float32), jax.ShapeDtypeStruct((n_pair, 1, seq), jnp.float32)] + [jax.ShapeDtypeStruct((heads * HD, toks), jnp.bfloat16)] * n_blk,
        compiler_params=pltpu.CompilerParams(dimension_semantics=("arbitrary", "arbitrary"), vmem_limit_bytes=48 * 1024 * 1024),
        cost_estimate=pl.CostEstimate(flops=n_pair * seq * seq * 2 * HD * 4, bytes_accessed=60000000, transcendentals=n_pair * seq * seq // 2),
        name="attn_fwd",
    )(me, cos_t, sin_t, bias_col, *slots)


def bwd_kernel(n_blk, coef, scale, me_ref, cos_ref, sin_ref, qkv_ref, out_ref, lse_ref, *refs):
    dctx = refs[:n_blk]
    dqkv_refs = refs[n_blk:2 * n_blk]
    db_ref = refs[2 * n_blk]
    k_nat, v_nat, do_t, delta, dq_acc, dk_acc, dv_acc = refs[2 * n_blk + 1:]
    me = me_ref[0]
    for s in range(n_blk):
        cols = pl.ds(pl.multiple_of(jnp.bitwise_xor(me, s) * BLK, BLK), BLK)
        d_rows = dctx[s][...]
        do_t[:, cols] = d_rows.astype(jnp.bfloat16)
        delta[:, cols] = jnp.sum(d_rows * out_ref[0, :, cols], axis=0, keepdims=True)
        k_nat[cols, :] = qkv_ref[0, HD:2 * HD, cols].T
        v_nat[cols, :] = qkv_ref[0, 2 * HD:3 * HD, cols].T
    dq_acc[...] = jnp.zeros_like(dq_acc)
    seq = n_blk * BLK
    n_k = seq // BK

    def tile(k_start, k_len, q_start, q_len, mask):
        k_sl = pl.ds(pl.multiple_of(k_start, SUB), k_len)
        q_sl = pl.ds(pl.multiple_of(q_start, SUB), q_len)
        q_t = qkv_ref[0, 0:HD, q_sl]
        g_t = do_t[:, q_sl]
        scores = nn_dot(k_nat[k_sl, :], q_t)
        d_probs = nn_dot(v_nat[k_sl, :], g_t)
        probs = jnp.exp2(scores * coef - lse_ref[0, :, q_sl])
        if mask is not None:
            probs = jnp.where(mask, probs, 0.0)
        d_scores = (probs * (d_probs - delta[:, q_sl])).astype(jnp.bfloat16)
        dv = nt_dot(g_t, probs.astype(jnp.bfloat16))
        dk = nt_dot(q_t, d_scores)
        dq_acc[:, q_sl] += nn_dot(qkv_ref[0, HD:2 * HD, k_sl], d_scores)
        return dk, dv

    tri = lax.broadcasted_iota(jnp.int32, (SUB, SUB), 0) <= lax.broadcasted_iota(jnp.int32, (SUB, SUB), 1)

    def one_k(j, _):
        base = j * BK
        dk0, dv0 = tile(base, SUB, base, SUB, tri)
        dk1, dv1 = tile(base + SUB, SUB, base + SUB, SUB, tri)
        dk2, dv2 = tile(base, SUB, base + SUB, SUB, None)
        start = (jnp.concatenate([dk0 + dk2, dk1], axis=1), jnp.concatenate([dv0 + dv2, dv1], axis=1))

        def one_q(i, carry):
            dk, dv = carry
            for c in range(BK // SUB):
                g_k, g_v = tile(base, BK, i * BK + c * SUB, SUB, None)
                dk, dv = dk + g_k, dv + g_v
            return dk, dv

        dk, dv = lax.fori_loop(j + 1, n_k, one_q, start)
        k_sl = pl.ds(pl.multiple_of(base, BK), BK)
        dk_acc[:, k_sl] = dk
        dv_acc[:, k_sl] = dv
        return 0

    lax.fori_loop(0, n_k, one_k, 0)
    lanes = jnp.zeros((3 * HD, 128), jnp.float32)
    for s in range(n_blk):
        cols = pl.ds(pl.multiple_of(jnp.bitwise_xor(me, s) * BLK, BLK), BLK)
        cos_t, sin_t = cos_ref[:, cols], -sin_ref[:, cols]
        g = jnp.concatenate([turn(dq_acc[:, cols] * scale, cos_t, sin_t), turn(dk_acc[:, cols] * scale, cos_t, sin_t), dv_acc[:, cols]], axis=0)
        dqkv_refs[s][...] = g.astype(jnp.bfloat16)
        for c in range(BLK // 128):
            lanes += g[:, c * 128:(c + 1) * 128]
    db_ref[0] = lanes


def attn_bwd(me, cos_t, sin_t, qkv, outs, lse, dctx, coef, scale, h_from, h_cnt):
    n_blk = len(dctx)
    rows, toks = dctx[0].shape
    batch, seq = toks // BLK, n_blk * BLK
    full = lambda h, b, me: (0, 0)
    hb_in = lambda h, b, me: (h + h_from, b)
    hb = lambda h, b, me: (h, b)
    one = lambda h, b, me: ((h + h_from) * batch + b, 0, 0)
    n_pair = h_cnt * batch
    return pl.pallas_call(
        lambda *refs: bwd_kernel(n_blk, coef, scale, *refs),
        grid_spec=pltpu.PrefetchScalarGridSpec(
            num_scalar_prefetch=1, grid=(h_cnt, batch),
            in_specs=[pl.BlockSpec((8, seq), full), pl.BlockSpec((8, seq), full), pl.BlockSpec((1, 3 * HD, seq), one), pl.BlockSpec((1, HD, seq), one), pl.BlockSpec((1, 1, seq), one)] + [pl.BlockSpec((HD, BLK), hb_in)] * n_blk,
            out_specs=[pl.BlockSpec((3 * HD, BLK), hb)] * n_blk + [pl.BlockSpec((1, 3 * HD, 128), lambda h, b, me: (h * batch + b, 0, 0))],
            scratch_shapes=[pltpu.VMEM((seq, HD), jnp.bfloat16), pltpu.VMEM((seq, HD), jnp.bfloat16), pltpu.VMEM((HD, seq), jnp.bfloat16), pltpu.VMEM((1, seq), jnp.float32)] + [pltpu.VMEM((HD, seq), jnp.float32)] * 3),
        out_shape=[jax.ShapeDtypeStruct((h_cnt * 3 * HD, toks), jnp.bfloat16)] * n_blk + [jax.ShapeDtypeStruct((n_pair, 3 * HD, 128), jnp.float32)],
        compiler_params=pltpu.CompilerParams(dimension_semantics=("arbitrary", "arbitrary"), vmem_limit_bytes=48 * 1024 * 1024),
        cost_estimate=pl.CostEstimate(flops=n_pair * seq * seq * 2 * HD * 10, bytes_accessed=80000000, transcendentals=n_pair * seq * seq // 2),
        name="attn_bwd",
    )(me, cos_t, sin_t, qkv, outs, lse, *dctx)


def norm_parts(rows):
    mean = jnp.mean(rows, axis=-1, keepdims=True)
    centered = rows - mean
    inv_std = lax.rsqrt(jnp.mean(centered * centered, axis=-1, keepdims=True) + EPS)
    return centered * inv_std, inv_std


def norm_backward(d_out, x_norm, inv_std, gain):
    d_norm = d_out * gain
    d_rows = inv_std * (d_norm - jnp.mean(d_norm, axis=-1, keepdims=True) - x_norm * jnp.mean(d_norm * x_norm, axis=-1, keepdims=True))
    return d_rows, jnp.sum(d_out * x_norm, axis=0), jnp.sum(d_out, axis=0)


def dot32(spec, lhs, rhs):
    return jnp.einsum(spec, lhs, rhs, preferred_element_type=jnp.float32)


def exact_gelu(pre_act):
    return jax.nn.gelu(pre_act, approximate=False)


def solution(mesh):
    n_cp = mesh.shape['cp']
    row_spec = P('dp', 'cp', None)
    in_specs = (row_spec, row_spec) + (P(),) * 12
    out_specs = (row_spec, row_spec, P('dp'), P('dp'), P('dp'), P('dp'), P('dp', None, None, None), P('dp', None, None), P('dp', None), P('dp'), P('dp', None), P('dp'), P('dp', None), P('dp'))

    def swap(value, mask):
        return lax.ppermute(value, 'cp', [(i, i ^ mask) for i in range(n_cp)])

    def local_layer(x_blk, dy_blk, ln1_gain, ln1_bias, ln2_gain, ln2_bias, w_qkv, b_qkv, w_out, b_out, w_up, b_up, w_down, b_down):
        batch, row_count, width = x_blk.shape
        heads, hd = w_qkv.shape[1], w_qkv.shape[3]
        ff = w_up.shape[1]
        toks, seq = batch * row_count, n_cp * row_count
        my_heads = heads // n_cp
        q_rows = my_heads * 3 * hd
        c_rows = my_heads * hd
        half = ff // 2
        scale = hd ** -0.5
        coef = scale * LOG2E
        me = lax.axis_index('cp')
        core = me % 2
        slot_of = [jnp.bitwise_xor(me, s) for s in range(n_cp)]
        bf = jnp.bfloat16

        x0 = x_blk.reshape(toks, width)
        dy32 = dy_blk.reshape(toks, width)
        g0 = dy32.astype(bf)
        x2 = swap(x0, 2)
        g2 = swap(g0, 2)
        x1 = swap(x0, 1)
        g1 = swap(g0, 1)
        x3 = swap(x2, 1)
        g3 = swap(g2, 1)
        xs, gs = [x0, x1, x2, x3], [g0, g1, g2, g3]

        w_t = jnp.transpose(w_qkv, (1, 2, 3, 0)).reshape(heads * 3 * hd, width)
        w_t_slot = [lax.dynamic_slice_in_dim(w_t, p * q_rows, q_rows, 0) for p in slot_of]
        w_o_slot = [lax.dynamic_slice_in_dim(w_out, p * c_rows, c_rows, 0) for p in slot_of]
        bias_col = lax.dynamic_slice_in_dim(b_qkv.astype(jnp.float32).reshape(heads * 3 * hd, 1), me * q_rows, q_rows, 0)
        inv_freq = ROPE_BASE ** (-2.0 * jnp.arange(8, dtype=jnp.float32) / 16)
        angles = inv_freq[:, None] * jnp.arange(seq, dtype=jnp.float32)[None, :]
        cos_t, sin_t = jnp.cos(angles), jnp.sin(angles)
        me_arr = me.astype(jnp.int32).reshape(1)

        h_in, m_in = [], []
        for s in range(n_cp):
            x_norm, inv_std = norm_parts(xs[s].astype(jnp.float32))
            h_in.append((x_norm * ln1_gain + ln1_bias).astype(bf))
            m_in.append((x_norm * ln2_gain + ln2_bias).astype(bf))
        slots = [dot32('cd,td->ct', w_t_slot[0], h_in[s]) for s in range(n_cp)]
        fwd = attn_fwd(me_arr, cos_t, sin_t, bias_col, slots, coef)
        qkv, outs, lse, ctx = fwd[0], fwd[1], fwd[2], fwd[3:]
        ctx_got = [ctx[0]] + [swap(ctx[s], s) for s in range(1, n_cp)]

        dctx = [dot32('ce,te->ct', w_o_slot[0], gs[s]) for s in range(n_cp)]
        dq_parts, db_parts = [], []
        for hh in range(my_heads):
            got = attn_bwd(me_arr, cos_t, sin_t, qkv, outs, lse, dctx, coef, scale, hh, 1)
            dq_parts.append(got[:n_cp])
            db_parts.append(jnp.sum(got[n_cp], axis=(0, 2)))
        dq_mine = [jnp.concatenate([dq_parts[hh][s] for hh in range(my_heads)], axis=0) for s in range(n_cp)]
        dq_got = [dq_mine[0]] + [jnp.concatenate([swap(dq_parts[hh][s], s) for hh in range(my_heads)], axis=0) for s in range(1, n_cp)]

        d_w_o = sum(dot32('ct,te->ce', ctx[s], gs[s]) for s in range(n_cp))
        d_w_t = sum(dot32('ct,td->cd', dq_mine[s], h_in[s]) for s in range(n_cp))

        def collect(mine):
            far = swap(mine, 2)
            near, diag = swap(mine, 1), swap(far, 1)
            rows = mine.shape[0]
            full = jnp.zeros((n_cp * rows,) + mine.shape[1:], mine.dtype)
            for s, part in enumerate((mine, near, far, diag)):
                full = lax.dynamic_update_slice_in_dim(full, part, slot_of[s] * rows, 0)
            return full

        d_w_out = collect(d_w_o)
        d_w_qkv_t = collect(d_w_t)
        d_w_qkv = jnp.transpose(d_w_qkv_t.reshape(heads, 3, hd, width), (3, 0, 1, 2))

        w_up_h = lax.dynamic_slice_in_dim(w_up, core * half, half, 1)
        w_down_h = lax.dynamic_slice_in_dim(w_down, core * half, half, 0)
        b_up_h = lax.dynamic_slice_in_dim(b_up, core * half, half, 0).astype(jnp.float32)
        d_w_up_h, d_w_down_h, db_up_h = 0.0, 0.0, 0.0
        mlp_part, dm_part = [], []
        for s in range(n_cp):
            up, = (dot32('td,df->tf', m_in[s], w_up_h) + b_up_h,)
            act, back = jax.vjp(exact_gelu, up)
            act_bf = act.astype(bf)
            d_up = back(dot32('td,fd->tf', gs[s], w_down_h))[0]
            d_up_bf = d_up.astype(bf)
            d_w_down_h += dot32('tf,td->fd', act_bf, gs[s])
            d_w_up_h += dot32('td,tf->df', m_in[s], d_up_bf)
            if s < 2:
                db_up_h += jnp.sum(d_up, axis=0)
                mlp_part.append(dot32('tf,fd->td', act_bf, w_down_h))
                dm_part.append(dot32('tf,df->td', d_up_bf, w_up_h))
        mlp = mlp_part[0] + swap(mlp_part[1], 1)
        d_m = dm_part[0] + swap(dm_part[1], 1)

        def pair_up(mine, axis):
            other = swap(mine, 1)
            shape = list(mine.shape)
            shape[axis] *= 2
            full = jnp.zeros(shape, mine.dtype)
            full = lax.dynamic_update_slice_in_dim(full, mine, core * half, axis)
            return lax.dynamic_update_slice_in_dim(full, other, (1 - core) * half, axis)

        d_w_up = pair_up(d_w_up_h, 1)
        d_w_down = pair_up(d_w_down_h, 0)

        x_rows = x0.astype(jnp.float32)
        proj = sum(dot32('ct,ce->te', ctx_got[s], w_o_slot[s]) for s in range(n_cp))
        y_rows = x_rows + (proj + b_out.astype(jnp.float32)) + (mlp + b_down.astype(jnp.float32))

        d_h = sum(dot32('ct,cd->td', dq_got[s], w_t_slot[s]) for s in range(n_cp))
        x_norm, inv_std = norm_parts(x_rows)
        dx1, dg1, db1 = norm_backward(d_h, x_norm, inv_std, ln1_gain)
        dx2, dg2, db2 = norm_backward(d_m, x_norm, inv_std, ln2_gain)
        dx = dy32 + dx1 + dx2

        db_qkv_mine = jnp.concatenate(db_parts)
        db_qkv = lax.dynamic_update_slice_in_dim(jnp.zeros((heads * 3 * hd,), jnp.float32), db_qkv_mine, me * q_rows, 0)
        db_up = lax.dynamic_update_slice_in_dim(jnp.zeros((ff,), jnp.float32), db_up_h, core * half, 0)
        small = lax.psum(jnp.concatenate([dg1, db1, dg2, db2, jnp.sum(dy32, axis=0), db_qkv, db_up]), 'cp')
        cut = [width, 2 * width, 3 * width, 4 * width, 5 * width, 5 * width + heads * 3 * hd]
        s_g1, s_b1, s_g2, s_b2, s_dy, s_bq, s_bu = jnp.split(small, cut)
        return (y_rows.astype(bf).reshape(x_blk.shape), dx.reshape(dy_blk.shape), s_g1, s_b1, s_g2, s_b2, d_w_qkv, s_bq.reshape(heads, 3, hd), d_w_out, s_dy, d_w_up, s_bu, d_w_down, s_dy)

    return jax.shard_map(local_layer, mesh=mesh, in_specs=in_specs, out_specs=out_specs, check_vma=False)
```

time: 3880 us -> 1430 us (0.37)
  waiting for transfers between devices: 1950 us -> 145 us
  starting transfers between devices: 903 us -> 21.9 us
  Pallas kernels: 0 us -> 412 us
  matrix products: 567 us -> 703 us
  local copies, waits for them, and re-layouts: 190 us -> 67 us
  other arithmetic: 179 us -> 56.7 us
  blocking collectives: 71.9 us -> 11.8 us
    ppermute x20 -> x31, waiting for transfers between devices: 1240 us -> 145 us  [swap(): return lax.ppermute(value, 'cp', [(i, i ^ mask) for i in range(n_cp)])]
    ppermute x20 -> x31, starting transfers between devices: 902 us -> 21.9 us  [swap(): return lax.ppermute(value, 'cp', [(i, i ^ mask) for i in range(n_cp)])]
    psum x1 -> x0, waiting for transfers between devices: 707 us -> none  [local_layer(): lax.psum((d_ln1_gain, d_ln1_bias, d_ln2_gain, d_ln2_bias, d_w_qkv, d_b_qk...]
    pallas_call x0 -> x5, Pallas kernels: none -> 412 us  [the longest x4 296 us: attn_bwd(): pl.pallas_call(lambda *refs: bwd_kernel(n_blk, coef, scale, *refs), grid_...]
    dot_general x18 -> x43, matrix products: 567 us -> 703 us  [dot32(): return jnp.einsum(spec, lhs, rhs, preferred_element_type=jnp.float32)]
    while x18 -> x0, local copies, waits for them, and re-layouts: 110 us -> none
    convert_element_type x3 -> x2, other arithmetic: 80.9 us -> 4.83 us  [the longest x1 4.82 us: local_layer(): h_in.append((x_norm * ln1_gain + ln1_bias).astype(bf))]
    psum x1, blocking collectives: 71.9 us -> 11.8 us  [local_layer(): lax.psum(jnp.concatenate([dg1, db1, dg2, db2, jnp.sum(dy32, axis=0), db_q...]
  transfers between devices with their start and end apart: 21 -> 31, of which waited for: 15 -> 6; matrix products, arithmetic and copies ran while one was open for 10% -> 57% of each run, Pallas kernels for 0% -> 29%
where the time goes in v1:
time: 1430 us; the launch traced here: 1420 us
  matrix products  703 us (49%)
  Pallas kernels  412 us (29%)
  waiting for transfers between devices  145 us (10%)
  local copies, waits for them, and re-layouts  67 us (5%)
  other arithmetic  56.7 us (4%)
  starting transfers between devices  21.9 us (2%)
    dot_general x43, matrix products, dot32(): return jnp.einsum(spec, lhs, rhs, preferred_element_type=jnp.float32)  703 us
    pallas_call x4, Pallas kernels, attn_bwd(): pl.pallas_call(lambda *refs: bwd_kernel(n_blk, coef, scale, *refs), grid_...  296 us
    ppermute x31, waiting for transfers between devices, swap(): return lax.ppermute(value, 'cp', [(i, i ^ mask) for i in range(n_cp)])  145 us
    pallas_call x1, Pallas kernels, attn_fwd(): pl.pallas_call(lambda *refs: fwd_kernel(n_blk, coef, *refs), grid_spec=pl...  115 us
  transfers between devices with their start and end apart: 31, of which 6 were waited for; matrix products, arithmetic and copies ran while one was open for 57% of the time, Pallas kernels for 29%

profile of v1, /device:TPU:0, one launch (start us, length us, event | category | flops | bytes accessed | tf_op | source)
XLA Modules:
  0.0 1419.5 jit_solution(6109307886284285749)
XLA Ops:
  38.8 29.5 %fusion.197 = f32[2048,2048]{1,0:T(8,128)} fusion(bf16[2048,1024]{1,0:T(8,128)(2,1)} %get-tuple-element.101, bf16[1024,4096]{1,0:T(8,128)(2,1)} %param.24, s32[]{:T(128)S(6)} %select_n.59), kind=kOutput, calls=%fused_computation.252 | convolution fusion | flops 8589934592 | bytes 25165828 | tf_op jit(solution)/shard_map/td,df->tf/dot_general | solution.py:252
  68.3 27.2 %collective-permute-done.1 = bf16[2048,1024]{1,0:T(8,128)(2,1)} collective-permute-done((bf16[2048,1024]{1,0:T(8,128)(2,1)}, bf16[2048,1024]{1,0:T(8,128)(2,1)}, u32[]{:S(2)}, u32[]{:S(2)}) %collective-permute-start.1) | collective-permute-done | bytes 4194336 | tf_op jit(solution)/shard_map/ppermute | solution.py:266
  121.9 125.1 %multiply_convert_fusion.2 = (bf16[2048,2048]{1,0:T(8,128)(2,1)}, f32[2048,2048]{1,0:T(8,128)}, f32[2048,2048]{1,0:T(8,128)}, bf16[2048,2048]{1,0:T(8,128)(2,1)}, f32[2048,2048]{1,0:T(8,128)}, /*index=5*/f32[2048,2048]{1,0:T(8,128)}) fusion(f32[2048]{0:T(1024)S(1)} %dynamic-slice_convert_fusion, f32[2048,2048]{1,0:T(8,128)} %fusion.191, ...), kind=kOutput, calls=%fused_computation.68 | convolution fusion | flops 9420406784 | bytes 125861888 | tf_op jit(solution)/shard_map/td,df->tf/dot_general | solution.py:252
  260.2 22.9 %fusion.301 = (f32[2048]{0:T(1024)S(1)}, bf16[2048,2048]{1,0:T(8,128)(2,1)}) fusion(f32[2048,2048]{1,0:T(8,128)} %get-tuple-element.95, bf16[2048,1024]{1,0:T(8,128)(2,1)} %collective-permute-done.7, bf16[4096,1024]{1,0:T(8,128)(2,1)} %param.26, s32[]{:T(128)S(6)} %select_n.59, f32[2048,2048]{1,0:T(8,128)} %get-tuple-element.114, ...), kind=kOutput, calls=%fused_computation.377 | convolution fusion | flops 8657041408 | bytes 50348036 | tf_op jit(solution)/shard_map/td,fd->tf/dot_general | solution.py:252
  297.8 23.1 %fusion.300 = (f32[2048]{0:T(1024)S(1)}, bf16[2048,2048]{1,0:T(8,128)(2,1)}) fusion(f32[2048,2048]{1,0:T(8,128)} %get-tuple-element.109, bf16[2048,1024]{1,0:T(8,128)(2,1)} %get-tuple-element.99, bf16[4096,1024]{1,0:T(8,128)(2,1)} %param.26, s32[]{:T(128)S(6)} %select_n.59, f32[2048,2048]{1,0:T(8,128)} %fusion.197, f32[2048]{0:T(1024)S(1)} %dynamic-slice_convert_fusion), kind=kOutput, calls=%fused_computation.376 | convolution fusion | flops 8657041408 | bytes 50348036 | tf_op jit(solution)/shard_map/td,fd->tf/dot_general | solution.py:252
  344.6 15.0 %fusion.306 = f32[2048,1024]{1,0:T(8,128)} fusion(bf16[2048,2048]{1,0:T(8,128)(2,1)} %get-tuple-element.108, bf16[2048,1024]{1,0:T(8,128)(2,1)} %get-tuple-element.99), kind=kOutput, calls=%fused_computation.380 | convolution fusion | flops 8589934592 | bytes 20971520 | tf_op jit(solution)/shard_map/tf,td->fd/dot_general | solution.py:252
  390.2 26.8 %fusion.366 = bf16[2048,2048]{1,0:T(8,128)(2,1)} fusion(f32[2048,2048]{1,0:T(8,128)} %get-tuple-element.107, f32[2048,2048]{1,0:T(8,128)} %fusion.191, f32[2048]{0:T(1024)S(1)} %dynamic-slice_convert_fusion, bf16[2048,1024]{1,0:T(8,128)(2,1)} %collective-permute-done.8, bf16[4096,1024]{1,0:T(8,128)(2,1)} %param.26, s32[]{:T(128)S(6)} %select_n.59), kind=kOutput, calls=%fused_computation.24.clone.clone.2 | convolution fusion | flops 8652849152 | bytes 50339844 | tf_op jit(solution)/shard_map/td,fd->tf/dot_general | solution.py:252
  417.1 15.6 %fusion.110 = f32[1024,2048]{1,0:T(8,128)} fusion(bf16[2048,1024]{1,0:T(8,128)(2,1)} %collective-permute-done.1, f32[1024]{0:T(1024)S(1)} %copy-done.54, f32[1024]{0:T(1024)S(1)} %copy-done.43, f32[2048]{0:T(1024)S(1)} %copy-done.69, f32[2048]{0:T(1024)S(1)} %copy-done.49, bf16[2048,2048]{1,0:T(8,128)(2,1)} %fusion.366), kind=kOutput, calls=%fused_computation.172 | convolution fusion | flops 8602517504 | bytes 20996096 | tf_op jit(solution)/shard_map/td,tf->df/dot_general | solution.py:252
  432.6 14.7 %fusion.307 = f32[2048,1024]{1,0:T(8,128)} fusion(bf16[2048,2048]{1,0:T(8,128)(2,1)} %get-tuple-element.94, bf16[2048,1024]{1,0:T(8,128)(2,1)} %collective-permute-done.7), kind=kOutput, calls=%fused_computation.381 | convolution fusion | flops 8589934592 | bytes 20971520 | tf_op jit(solution)/shard_map/tf,td->fd/dot_general | solution.py:252
  459.2 19.2 %fusion.104 = f32[2048,1024]{1,0:T(8,128)} fusion(bf16[2048,1024]{1,0:T(8,128)(2,1)} %collective-permute-done.8, f32[2048,2048]{1,0:T(8,128)} %get-tuple-element.107, f32[2048,2048]{1,0:T(8,128)} %fusion.191, f32[2048]{0:T(1024)S(1)} %dynamic-slice_convert_fusion), kind=kOutput, calls=%fused_computation.162 | convolution fusion | flops 8606711808 | bytes 46145536 | tf_op jit(solution)/shard_map/tf,td->fd/dot_general | solution.py:252
  493.8 115.3 %attn_fwd.1 = (bf16[8,192,4096]{2,1,0:T(8,128)(2,1)}, f32[8,64,4096]{2,1,0:T(8,128)}, f32[8,1,4096]{2,1,0:T(1,128)S(1)}, bf16[256,2048]{1,0:T(8,128)(2,1)S(1)}, ...) custom-call(s32[1]{0:T(128)} %bitcast.1.refs_0_, f32[8,4096]{1,0:T(8,128)S(1)} %copy-done.7, ...), custom_call_target="tpu_custom_call" | custom-call | flops 68719476736 | bytes 60000000 | tf_op jit(solution)/shard_map/attn_fwd/pallas_call | solution.py:134
  615.3 74.0 %attn_bwd.7 = (bf16[192,2048]{1,0:T(8,128)(2,1)S(1)}, bf16[192,2048]{1,0:T(8,128)(2,1)S(1)}, bf16[192,2048]{1,0:T(8,128)(2,1)}, bf16[192,2048]{1,0:T(8,128)(2,1)S(1)}, f32[2,192,128]{2,1,0:T(8,128)S(1)}) custom-call(s32[1]{0:T(128)} %bitcast.1.refs_0_, f32[8,4096]{1,0:T(8,128)S(1)} %copy-done.7, f32[8,4096]{1,0:T(8,128)S(1)} %copy-done.6, ...), custom_call_target="tpu_custom_call" | custom-call | flops 42949672960 | bytes 80000000 | tf_op jit(solution)/shard_map/attn_bwd/pallas_call | solution.py:224
  691.1 74.1 %attn_bwd.6 = (bf16[192,2048]{1,0:T(8,128)(2,1)S(1)}, bf16[192,2048]{1,0:T(8,128)(2,1)S(1)}, bf16[192,2048]{1,0:T(8,128)(2,1)}, bf16[192,2048]{1,0:T(8,128)(2,1)S(1)}, f32[2,192,128]{2,1,0:T(8,128)S(1)}) custom-call(s32[1]{0:T(128)} %bitcast.1.refs_0_, f32[8,4096]{1,0:T(8,128)S(1)} %copy-done.7, f32[8,4096]{1,0:T(8,128)S(1)} %copy-done.6, ...), custom_call_target="tpu_custom_call" | custom-call | flops 42949672960 | bytes 80000000 | tf_op jit(solution)/shard_map/attn_bwd/pallas_call | solution.py:224
  767.0 74.1 %attn_bwd.5 = (bf16[192,2048]{1,0:T(8,128)(2,1)S(1)}, bf16[192,2048]{1,0:T(8,128)(2,1)}, bf16[192,2048]{1,0:T(8,128)(2,1)}, bf16[192,2048]{1,0:T(8,128)(2,1)S(1)}, f32[2,192,128]{2,1,0:T(8,128)S(1)}) custom-call(s32[1]{0:T(128)} %bitcast.1.refs_0_, f32[8,4096]{1,0:T(8,128)S(1)} %copy-done.7, f32[8,4096]{1,0:T(8,128)S(1)} %copy-done.6, ...), custom_call_target="tpu_custom_call" | custom-call | flops 42949672960 | bytes 80000000 | tf_op jit(solution)/shard_map/attn_bwd/pallas_call | solution.py:224
  842.6 74.2 %attn_bwd.4 = (bf16[192,2048]{1,0:T(8,128)(2,1)S(1)}, bf16[192,2048]{1,0:T(8,128)(2,1)}, bf16[192,2048]{1,0:T(8,128)(2,1)}, bf16[192,2048]{1,0:T(8,128)(2,1)S(1)}, f32[2,192,128]{2,1,0:T(8,128)S(1)}) custom-call(s32[1]{0:T(128)} %bitcast.1.refs_0_, f32[8,4096]{1,0:T(8,128)S(1)} %copy-done.7, f32[8,4096]{1,0:T(8,128)S(1)} %copy-done.6, ...), custom_call_target="tpu_custom_call" | custom-call | flops 42949672960 | bytes 80000000 | tf_op jit(solution)/shard_map/attn_bwd/pallas_call | solution.py:224
  938.4 15.6 %fusion.189 = f32[2048,2048]{1,0:T(8,128)} fusion(bf16[1024,4096]{1,0:T(8,128)(2,1)} %param.24, s32[]{:T(128)S(6)} %select_n.59, bf16[2048,1024]{1,0:T(8,128)(2,1)} %collective-permute-done.2, f32[1024]{0:T(1024)S(1)} %copy-done.55, f32[1024]{0:T(1024)S(1)} %copy-done.44, f32[2048]{0:T(1024)S(1)} %copy-done.52, f32[2048]{0:T(1024)S(1)} %copy-done.37), kind=kOutput, calls=%fused_computation.244 | convolution fusion | flops 8602517504 | bytes 25190404 | tf_op jit(solution)/shard_map/td,df->tf/dot_general | solution.py:252
  967.3 48.8 %constant_dynamic-update-slice_fusion.6 = (f32[4096,1024]{1,0:T(8,128)}, f32[2048,1024]{1,0:T(8,128)}) fusion(f32[4096,1024]{1,0:T(8,128)} %broadcast_in_dim.17, s32[]{:T(128)S(6)} %select_n.59, bf16[2048,1024]{1,0:T(8,128)(2,1)} %collective-permute-done.9, f32[2048,2048]{1,0:T(8,128)} %fusion.189, f32[2048]{0:T(1024)S(1)} %copy-done.66, ...), kind=kOutput, calls=%fused_computation.320 | convolution fusion | flops 8873050112 | bytes 62922756 | tf_op jit(solution)/shard_map/tf,td->fd/dot_general | solution.py:252
  1024.4 63.6 %constant_dynamic-update-slice_fusion.8 = (f32[1024,4096]{1,0:T(8,128)}, f32[1024,2048]{1,0:T(8,128)}) fusion(f32[1024,4096]{1,0:T(8,128)} %broadcast_in_dim.16, s32[]{:T(128)S(6)} %select_n.59, f32[2048,2048]{1,0:T(8,128)} %fusion.189, f32[2048]{0:T(1024)} %copy-done.65, bf16[2048,1024]{1,0:T(8,128)(2,1)} %collective-permute-done.9, ...), kind=kOutput, calls=%fused_computation.322 | convolution fusion | flops 17492344832 | bytes 71312384 | tf_op jit(solution)/shard_map/td,tf->df/dot_general | solution.py:252
  1179.8 69.0 %collective-permute-done.27 = f32[256,1024]{1,0:T(8,128)S(1)} collective-permute-done((f32[256,1024]{1,0:T(8,128)S(1)}, f32[256,1024]{1,0:T(8,128)S(1)}, u32[]{:S(2)}, u32[]{:S(2)}) %collective-permute-start.27) | collective-permute-done | bytes 1048608 | tf_op jit(solution)/shard_map/ppermute | solution.py:266
  1272.9 14.9 %fusion.122 = f32[2048,1024]{1,0:T(8,128)} fusion(f32[2048,1024]{1,0:T(8,128)} %collective-permute-done.22, bf16[2048,2048]{1,0:T(8,128)(2,1)} %get-tuple-element.117, bf16[1024,4096]{1,0:T(8,128)(2,1)S(1)} %bitcast.171, s32[]{:T(128)S(6)} %select_n.59), kind=kOutput, calls=%fused_computation.184 | convolution fusion | flops 8592031744 | bytes 29360132 | tf_op jit(solution)/shard_map/tf,df->td/dot_general | solution.py:252
  1297.3 16.1 %collective-permute-done.19 = bf16[192,2048]{1,0:T(8,128)(2,1)S(1)} collective-permute-done((bf16[192,2048]{1,0:T(8,128)(2,1)S(1)}, bf16[192,2048]{1,0:T(8,128)(2,1)S(1)}, u32[]{:S(2)}, u32[]{:S(2)}) %collective-permute-start.19) | collective-permute-done | bytes 786464 | tf_op jit(solution)/shard_map/ppermute | solution.py:266
  1314.1 16.1 %collective-permute-done.18 = bf16[192,2048]{1,0:T(8,128)(2,1)S(1)} collective-permute-done((bf16[192,2048]{1,0:T(8,128)(2,1)S(1)}, bf16[192,2048]{1,0:T(8,128)(2,1)S(1)}, u32[]{:S(2)}, u32[]{:S(2)}) %collective-permute-start.18) | collective-permute-done | bytes 786464 | tf_op jit(solution)/shard_map/ppermute | solution.py:266
  1332.0 18.7 %fusion.98 = (f32[1024]{0:T(1024)S(1)}, f32[2048]{0:T(1024)S(1)}, f32[2048]{0:T(1024)S(1)}, f32[1024]{0:T(1024)S(1)}, f32[1024]{0:T(1024)S(1)}, /*index=5*/f32[2...) fusion(f32[2048]{0:T(1024)S(1)} %copy-done.40, f32[2048]{0:T(1024)S(1)} %copy-done.42, ...), kind=kOutput, calls=%fused_computation.156 | convolution fusion | flops 3275739136 | bytes 50929668 | tf_op jit(solution)/shard_map/ct,cd->td/dot_general | solution.py:252
  1380.0 18.3 %fusion.101 = bf16[2048,1024]{1,0:T(8,128)(2,1)} fusion(bf16[2048,1024]{1,0:T(8,128)(2,1)} %bitcast.162, f32[2048,1024]{1,0:T(8,128)} %fusion.187, f32[2048,1024]{1,0:T(8,128)} %collective-permute-done.6, f32[2048,1024]{1,0:T(8,128)} %fusion.218, f32[2048,1024]{1,0:T(8,128)} %fusion.230, f32[2048,1024]{1,0:T(8,128)} %fusion.220, f32[1024]{0:T(1024)S(1)} %copy-done.61, ...), kind=kOutput, calls=%fused_computation.159 | convolution fusion | flops 1094713344 | bytes 51912708 | tf_op jit(solution)/shard_map/ct,ce->te/dot_general | solution.py:252
  (376 shorter events, 405.1 us)
Async XLA Ops:
  0.7 94.8 %collective-permute-start.1 = (bf16[2048,1024]{1,0:T(8,128)(2,1)}, bf16[2048,1024]{1,0:T(8,128)(2,1)}, u32[]{:S(2)}, u32[]{:S(2)}) collective-permute-start(bf16[2048,1024]{1,0:T(8,128)(2,1)} %bitcast.160), channel_id=1, source_target_pairs={{0,2},{1,3},{2,0},{3,1},{4,6},{5,7},{6,4},{7,5}} | collective-permute-start | bytes 12582920 | tf_op jit(solution)/shard_map/ppermute | solution.py:266
  4.1 97.3 %collective-permute-start = (bf16[2048,1024]{1,0:T(8,128)(2,1)}, bf16[2048,1024]{1,0:T(8,128)(2,1)}, u32[]{:S(2)}, u32[]{:S(2)}) collective-permute-start(bf16[2048,1024]{1,0:T(8,128)(2,1)} %bitcast.161), channel_id=1, source_target_pairs={{0,1},{1,0},{2,3},{3,2},{4,5},{5,4},{6,7},{7,6}} | collective-permute-start | bytes 12582920 | tf_op jit(solution)/shard_map/ppermute | solution.py:266
  11.1 249.2 %collective-permute-start.7 = (bf16[2048,1024]{1,0:T(8,128)(2,1)}, bf16[2048,1024]{1,0:T(8,128)(2,1)}, u32[]{:S(2)}, u32[]{:S(2)}) collective-permute-start(bf16[2048,1024]{1,0:T(8,128)(2,1)} %get-tuple-element.99), channel_id=1, source_target_pairs={{0,1},{1,0},{2,3},{3,2},{4,5},{5,4},{6,7},{7,6}} | collective-permute-start | bytes 12582920 | tf_op jit(solution)/shard_map/ppermute | solution.py:266
  11.6 359.6 %collective-permute-start.8 = (bf16[2048,1024]{1,0:T(8,128)(2,1)}, bf16[2048,1024]{1,0:T(8,128)(2,1)}, u32[]{:S(2)}, u32[]{:S(2)}) collective-permute-start(bf16[2048,1024]{1,0:T(8,128)(2,1)} %get-tuple-element.99), channel_id=1, source_target_pairs={{0,2},{1,3},{2,0},{3,1},{4,6},{5,7},{6,4},{7,5}} | collective-permute-start | bytes 12582920 | tf_op jit(solution)/shard_map/ppermute | solution.py:266
  297.8 974.7 %collective-permute-start.22 = (f32[2048,1024]{1,0:T(8,128)}, f32[2048,1024]{1,0:T(8,128)}, u32[]{:S(2)}, u32[]{:S(2)}) collective-permute-start(f32[2048,1024]{1,0:T(8,128)} %fusion.116), channel_id=1, source_target_pairs={{0,1},{1,0},{2,3},{3,2},{4,5},{5,4},{6,7},{7,6}} | collective-permute-start | bytes 25165832 | tf_op jit(solution)/shard_map/ppermute | solution.py:266
  339.2 139.3 %collective-permute-start.2 = (bf16[2048,1024]{1,0:T(8,128)(2,1)}, bf16[2048,1024]{1,0:T(8,128)(2,1)}, u32[]{:S(2)}, u32[]{:S(2)}) collective-permute-start(bf16[2048,1024]{1,0:T(8,128)(2,1)} %collective-permute-done.1), channel_id=1, source_target_pairs={{0,1},{1,0},{2,3},{3,2},{4,5},{5,4},{6,7},{7,6}} | collective-permute-start | bytes 12582920 | tf_op jit(solution)/shard_map/ppermute | solution.py:266
  375.9 234.2 %collective-permute-start.9 = (bf16[2048,1024]{1,0:T(8,128)(2,1)}, bf16[2048,1024]{1,0:T(8,128)(2,1)}, u32[]{:S(2)}, u32[]{:S(2)}) collective-permute-start(bf16[2048,1024]{1,0:T(8,128)(2,1)} %collective-permute-done.8), channel_id=1, source_target_pairs={{0,1},{1,0},{2,3},{3,2},{4,5},{5,4},{6,7},{7,6}} | collective-permute-start | bytes 12582920 | tf_op jit(solution)/shard_map/ppermute | solution.py:266
  916.9 208.0 %collective-permute-start.17 = (bf16[192,2048]{1,0:T(8,128)(2,1)}, bf16[192,2048]{1,0:T(8,128)(2,1)}, u32[]{:S(2)}, u32[]{:S(2)}) collective-permute-start(bf16[192,2048]{1,0:T(8,128)(2,1)} %get-tuple-element.59), channel_id=1, source_target_pairs={{0,2},{1,3},{2,0},{3,1},{4,6},{5,7},{6,4},{7,5}} | collective-permute-start | bytes 2359304 | tf_op jit(solution)/shard_map/ppermute | solution.py:266
  919.0 206.0 %collective-permute-start.16 = (bf16[192,2048]{1,0:T(8,128)(2,1)}, bf16[192,2048]{1,0:T(8,128)(2,1)}, u32[]{:S(2)}, u32[]{:S(2)}) collective-permute-start(bf16[192,2048]{1,0:T(8,128)(2,1)} %get-tuple-element.58), channel_id=1, source_target_pairs={{0,2},{1,3},{2,0},{3,1},{4,6},{5,7},{6,4},{7,5}} | collective-permute-start | bytes 2359304 | tf_op jit(solution)/shard_map/ppermute | solution.py:266
  919.0 210.3 %collective-permute-start.15 = (bf16[192,2048]{1,0:T(8,128)(2,1)}, bf16[192,2048]{1,0:T(8,128)(2,1)}, u32[]{:S(2)}, u32[]{:S(2)}) collective-permute-start(bf16[192,2048]{1,0:T(8,128)(2,1)} %get-tuple-element.57), channel_id=1, source_target_pairs={{0,2},{1,3},{2,0},{3,1},{4,6},{5,7},{6,4},{7,5}} | collective-permute-start | bytes 2359304 | tf_op jit(solution)/shard_map/ppermute | solution.py:266
  921.0 208.4 %collective-permute-start.14 = (bf16[192,2048]{1,0:T(8,128)(2,1)}, bf16[192,2048]{1,0:T(8,128)(2,1)}, u32[]{:S(2)}, u32[]{:S(2)}) collective-permute-start(bf16[192,2048]{1,0:T(8,128)(2,1)} %get-tuple-element.56), channel_id=1, source_target_pairs={{0,2},{1,3},{2,0},{3,1},{4,6},{5,7},{6,4},{7,5}} | collective-permute-start | bytes 2359304 | tf_op jit(solution)/shard_map/ppermute | solution.py:266
  1135.6 126.0 %collective-permute-start.23 = (f32[768,1024]{1,0:T(8,128)}, f32[768,1024]{1,0:T(8,128)}, u32[]{:S(2)}, u32[]{:S(2)}) collective-permute-start(f32[768,1024]{1,0:T(8,128)} %get-tuple-element.121), channel_id=1, source_target_pairs={{0,1},{1,0},{2,3},{3,2},{4,5},{5,4},{6,7},{7,6}} | collective-permute-start | bytes 9437192 | tf_op jit(solution)/shard_map/ppermute | solution.py:266
  1146.1 121.1 %collective-permute-start.24 = (f32[768,1024]{1,0:T(8,128)}, f32[768,1024]{1,0:T(8,128)}, u32[]{:S(2)}, u32[]{:S(2)}) collective-permute-start(f32[768,1024]{1,0:T(8,128)} %get-tuple-element.121), channel_id=1, source_target_pairs={{0,2},{1,3},{2,0},{3,1},{4,6},{5,7},{6,4},{7,5}} | collective-permute-start | bytes 9437192 | tf_op jit(solution)/shard_map/ppermute | solution.py:266
  1159.7 89.2 %collective-permute-start.27 = (f32[256,1024]{1,0:T(8,128)S(1)}, f32[256,1024]{1,0:T(8,128)S(1)}, u32[]{:S(2)}, u32[]{:S(2)}) collective-permute-start(f32[256,1024]{1,0:T(8,128)S(1)} %copy-done.34), channel_id=1, source_target_pairs={{0,2},{1,3},{2,0},{3,1},{4,6},{5,7},{6,4},{7,5}} | collective-permute-start | bytes 3145736 | tf_op jit(solution)/shard_map/ppermute | solution.py:266
  1170.8 84.1 %collective-permute-start.3 = (bf16[256,2048]{1,0:T(8,128)(2,1)S(1)}, bf16[256,2048]{1,0:T(8,128)(2,1)S(1)}, u32[]{:S(2)}, u32[]{:S(2)}) collective-permute-start(bf16[256,2048]{1,0:T(8,128)(2,1)S(1)} %copy-done.10), channel_id=1, source_target_pairs={{0,1},{1,0},{2,3},{3,2},{4,5},{5,4},{6,7},{7,6}} | collective-permute-start | bytes 3145736 | tf_op jit(solution)/shard_map/ppermute | solution.py:266
  1255.0 125.0 %collective-permute-start.6 = (f32[2048,1024]{1,0:T(8,128)}, f32[2048,1024]{1,0:T(8,128)}, u32[]{:S(2)}, u32[]{:S(2)}) collective-permute-start(f32[2048,1024]{1,0:T(8,128)} %fusion.185), channel_id=1, source_target_pairs={{0,1},{1,0},{2,3},{3,2},{4,5},{5,4},{6,7},{7,6}} | collective-permute-start | bytes 25165832 | tf_op jit(solution)/shard_map/ppermute | solution.py:266
  1260.1 27.6 %collective-permute-start.21 = (bf16[192,2048]{1,0:T(8,128)(2,1)S(1)}, bf16[192,2048]{1,0:T(8,128)(2,1)S(1)}, u32[]{:S(2)}, u32[]{:S(2)}) collective-permute-start(bf16[192,2048]{1,0:T(8,128)(2,1)S(1)} %copy-done.22), channel_id=1, source_target_pairs={{0,3},{1,2},{2,1},{3,0},{4,7},{5,6},{6,5},{7,4}} | collective-permute-start | bytes 2359304 | tf_op jit(solution)/shard_map/ppermute | solution.py:266
  1261.7 34.9 %collective-permute-start.20 = (bf16[192,2048]{1,0:T(8,128)(2,1)S(1)}, bf16[192,2048]{1,0:T(8,128)(2,1)S(1)}, u32[]{:S(2)}, u32[]{:S(2)}) collective-permute-start(bf16[192,2048]{1,0:T(8,128)(2,1)S(1)} %copy-done.19), channel_id=1, source_target_pairs={{0,3},{1,2},{2,1},{3,0},{4,7},{5,6},{6,5},{7,4}} | collective-permute-start | bytes 2359304 | tf_op jit(solution)/shard_map/ppermute | solution.py:266
  1267.1 46.3 %collective-permute-start.19 = (bf16[192,2048]{1,0:T(8,128)(2,1)S(1)}, bf16[192,2048]{1,0:T(8,128)(2,1)S(1)}, u32[]{:S(2)}, u32[]{:S(2)}) collective-permute-start(bf16[192,2048]{1,0:T(8,128)(2,1)S(1)} %copy-done.16), channel_id=1, source_target_pairs={{0,3},{1,2},{2,1},{3,0},{4,7},{5,6},{6,5},{7,4}} | collective-permute-start | bytes 2359304 | tf_op jit(solution)/shard_map/ppermute | solution.py:266
  1272.5 57.8 %collective-permute-start.18 = (bf16[192,2048]{1,0:T(8,128)(2,1)S(1)}, bf16[192,2048]{1,0:T(8,128)(2,1)S(1)}, u32[]{:S(2)}, u32[]{:S(2)}) collective-permute-start(bf16[192,2048]{1,0:T(8,128)(2,1)S(1)} %copy-done.13), channel_id=1, source_target_pairs={{0,3},{1,2},{2,1},{3,0},{4,7},{5,6},{6,5},{7,4}} | collective-permute-start | bytes 2359304 | tf_op jit(solution)/shard_map/ppermute | solution.py:266
  1287.8 92.1 %collective-permute-start.5 = (bf16[256,2048]{1,0:T(8,128)(2,1)S(1)}, bf16[256,2048]{1,0:T(8,128)(2,1)}, u32[]{:S(2)}, u32[]{:S(2)}) collective-permute-start(bf16[256,2048]{1,0:T(8,128)(2,1)S(1)} %copy-done.3), channel_id=1, source_target_pairs={{0,3},{1,2},{2,1},{3,0},{4,7},{5,6},{6,5},{7,4}} | collective-permute-start | bytes 3145736 | tf_op jit(solution)/shard_map/ppermute | solution.py:266
  1296.6 105.7 %collective-permute-start.29 = (f32[1024,2048]{1,0:T(8,128)}, f32[1024,2048]{1,0:T(8,128)}, u32[]{:S(2)}, u32[]{:S(2)}) collective-permute-start(f32[1024,2048]{1,0:T(8,128)} %get-tuple-element.125), channel_id=1, source_target_pairs={{0,1},{1,0},{2,3},{3,2},{4,5},{5,4},{6,7},{7,6}} | collective-permute-start | bytes 25165832 | tf_op jit(solution)/shard_map/ppermute | solution.py:266
  1313.4 96.7 %collective-permute-start.30 = (f32[2048,1024]{1,0:T(8,128)}, f32[2048,1024]{1,0:T(8,128)}, u32[]{:S(2)}, u32[]{:S(2)}) collective-permute-start(f32[2048,1024]{1,0:T(8,128)} %get-tuple-element.127), channel_id=1, source_target_pairs={{0,1},{1,0},{2,3},{3,2},{4,5},{5,4},{6,7},{7,6}} | collective-permute-start | bytes 25165832 | tf_op jit(solution)/shard_map/ppermute | solution.py:266
  1331.2 67.1 %collective-permute-start.25 = (f32[768,1024]{1,0:T(8,128)}, f32[768,1024]{1,0:T(8,128)}, u32[]{:S(2)}, u32[]{:S(2)}) collective-permute-start(f32[768,1024]{1,0:T(8,128)} %collective-permute-done.24), channel_id=1, source_target_pairs={{0,1},{1,0},{2,3},{3,2},{4,5},{5,4},{6,7},{7,6}} | collective-permute-start | bytes 9437192 | tf_op jit(solution)/shard_map/ppermute | solution.py:266
  (112 other events, 2972.6 us)

commit v2 on v1

v2 whole, which is shorter than its diff:
```python
import functools
import jax
import jax.numpy as jnp
from jax import lax
from jax.experimental import pallas as pl
from jax.experimental.pallas import tpu as pltpu
from jax.sharding import PartitionSpec as P

EPS = 1e-5
ROPE_BASE = 10000.0

NEG_BIG = -1e30
LOG2E = 1.4426950408889634
HD = 64
TRIO = 3 * HD
Q_ROWS = slice(HD)
K_ROWS = slice(HD, 2 * HD)
V_ROWS = slice(2 * HD, TRIO)
VMEM_GRANT = 56 << 20
BLK = 1024
SUB = 256
BK = 512


def nn_dot(lhs, rhs):
    return lax.dot_general(lhs, rhs, (((1,), (0,)), ((), ())), preferred_element_type=jnp.float32)


def nt_dot(lhs, rhs):
    return lax.dot_general(lhs, rhs, (((1,), (1,)), ((), ())), preferred_element_type=jnp.float32)


def turn(rows, cos_t, sin_t):
    lo, hi = rows[0:8], rows[8:16]
    return jnp.concatenate([lo * cos_t - hi * sin_t, hi * cos_t + lo * sin_t, rows[16:]], axis=0)


def fwd_kernel(n_blk, coef, me_ref, cos_ref, sin_ref, bias_ref, *refs):
    slots = refs[:n_blk]
    qkv_ref, out_ref, lse_ref = refs[n_blk:n_blk + 3]
    ctx_refs = refs[n_blk + 3:2 * n_blk + 3]
    k_nat, s_a, s_b = refs[2 * n_blk + 3:]
    me = me_ref[0]
    bias = bias_ref[...]
    for s in range(n_blk):
        cols = pl.ds(pl.multiple_of(jnp.bitwise_xor(me, s) * BLK, BLK), BLK)
        cos_t, sin_t = cos_ref[:, cols], sin_ref[:, cols]
        rows = slots[s][...] + bias
        q_t = turn(rows[Q_ROWS], cos_t, sin_t)
        k_t = turn(rows[K_ROWS], cos_t, sin_t)
        qkv_ref[0, Q_ROWS, cols] = q_t.astype(jnp.bfloat16)
        qkv_ref[0, K_ROWS, cols] = k_t.astype(jnp.bfloat16)
        qkv_ref[0, V_ROWS, cols] = rows[V_ROWS].astype(jnp.bfloat16)
        k_nat[cols, :] = k_t.T.astype(jnp.bfloat16)

    n_sub = BLK // SUB

    def q_cols(q_idx, sub):
        return pl.ds(pl.multiple_of(q_idx * BLK + sub * SUB, SUB), SUB)

    def make(q_idx, k_start, sub, k_len):
        scores = nn_dot(k_nat[pl.ds(pl.multiple_of(k_start, SUB), k_len), :], qkv_ref[0, Q_ROWS, q_cols(q_idx, sub)])
        return scores

    def put(q_idx, k_start, sub, buf):
        scores = make(q_idx, k_start, sub, BK)
        buf[:, sub * SUB:(sub + 1) * SUB] = scores
        return jnp.max(scores, axis=0, keepdims=True)

    def take(state, top, k_start, scores):
        old_max, tot, acc = state
        new_max = jnp.maximum(old_max, top)
        probs = jnp.exp2((scores - new_max) * coef)
        fade = jnp.exp2((old_max - new_max) * coef)
        tot = tot * fade + jnp.sum(probs, axis=0, keepdims=True)
        v_t = qkv_ref[0, V_ROWS, pl.ds(pl.multiple_of(k_start, SUB), scores.shape[0])]
        acc = acc * fade + nn_dot(v_t, probs.astype(jnp.bfloat16))
        return new_max, tot, acc

    def one_q(q_idx, _):
        base = q_idx * BLK
        tops = tuple(put(q_idx, 0, c, s_a) for c in range(n_sub))
        start = tuple((jnp.full((1, SUB), NEG_BIG, jnp.float32), jnp.zeros((1, SUB), jnp.float32), jnp.zeros((HD, SUB), jnp.float32)) for _ in range(n_sub))

        def pair(j, carry):
            states, tops_a = carry
            k0 = j * (2 * BK)
            tops_b, mid = [], []
            for c in range(n_sub):
                tops_b.append(put(q_idx, k0 + BK, c, s_b))
                mid.append(take(states[c], tops_a[c], k0, s_a[:, c * SUB:(c + 1) * SUB]))
            tops_n, fin = [], []
            for c in range(n_sub):
                tops_n.append(put(q_idx, k0 + 2 * BK, c, s_a))
                fin.append(take(mid[c], tops_b[c], k0 + BK, s_b[:, c * SUB:(c + 1) * SUB]))
            return tuple(fin), tuple(tops_n)

        states, tops = lax.fori_loop(0, q_idx, pair, (start, tops))
        states = list(states)
        tri = lax.broadcasted_iota(jnp.int32, (SUB, SUB), 0) <= lax.broadcasted_iota(jnp.int32, (SUB, SUB), 1)

        def masked(scores):
            return jnp.where(tri, scores, NEG_BIG)

        half = n_sub // 2
        for c in range(n_sub):
            if c < half:
                for r in range(c):
                    part = s_a[r * SUB:(r + 1) * SUB, c * SUB:(c + 1) * SUB]
                    states[c] = take(states[c], jnp.max(part, axis=0, keepdims=True), base + r * SUB, part)
                part = masked(s_a[c * SUB:(c + 1) * SUB, c * SUB:(c + 1) * SUB])
                states[c] = take(states[c], jnp.max(part, axis=0, keepdims=True), base + c * SUB, part)
            else:
                states[c] = take(states[c], tops[c], base, s_a[:, c * SUB:(c + 1) * SUB])
                for r in range(half, c + 1):
                    part = make(q_idx, base + r * SUB, c, SUB)
                    if r == c:
                        part = masked(part)
                    states[c] = take(states[c], jnp.max(part, axis=0, keepdims=True), base + r * SUB, part)
        for c in range(n_sub):
            top, tot, acc = states[c]
            outs = acc / tot
            out_ref[0, :, q_cols(q_idx, c)] = outs
            lse_ref[0, :, q_cols(q_idx, c)] = top * coef + jnp.log2(tot)
        return 0

    lax.fori_loop(0, n_blk, one_q, 0)
    for s in range(n_blk):
        cols = pl.ds(pl.multiple_of(jnp.bitwise_xor(me, s) * BLK, BLK), BLK)
        ctx_refs[s][...] = out_ref[0, :, cols].astype(jnp.bfloat16)


def attn_fwd(me, cos_t, sin_t, bias_col, slots, coef):
    n_blk = len(slots)
    rows, toks = slots[0].shape
    heads, batch, seq = rows // (TRIO), toks // BLK, n_blk * BLK
    n_pair = heads * batch
    full = lambda h, b, me: (0, 0)
    hb = lambda h, b, me: (h, b)
    one = lambda h, b, me: (h * batch + b, 0, 0)
    return pl.pallas_call(
        lambda *refs: fwd_kernel(n_blk, coef, *refs),
        grid_spec=pltpu.PrefetchScalarGridSpec(
            num_scalar_prefetch=1, grid=(heads, batch),
            in_specs=[*[pl.BlockSpec((8, seq), full)] * 2, pl.BlockSpec((TRIO, 1), lambda h, b, me: (h, 0))] + [pl.BlockSpec((TRIO, BLK), hb)] * n_blk,
            out_specs=[pl.BlockSpec((1, TRIO, seq), one), pl.BlockSpec((1, HD, seq), one), pl.BlockSpec((1, 1, seq), one)] + [pl.BlockSpec((HD, BLK), hb)] * n_blk,
            scratch_shapes=[pltpu.VMEM((seq, HD), jnp.bfloat16), pltpu.VMEM((BK, BLK), jnp.float32), pltpu.VMEM((BK, BLK), jnp.float32)]),
        out_shape=[jax.ShapeDtypeStruct((n_pair, TRIO, seq), jnp.bfloat16), jax.ShapeDtypeStruct((n_pair, HD, seq), jnp.float32), jax.ShapeDtypeStruct((n_pair, 1, seq), jnp.float32)] + [jax.ShapeDtypeStruct((heads * HD, toks), jnp.bfloat16)] * n_blk,
        compiler_params=pltpu.CompilerParams(dimension_semantics=("arbitrary", "arbitrary"), vmem_limit_bytes=VMEM_GRANT),
        cost_estimate=pl.CostEstimate(flops=n_pair * seq * seq * 2 * HD * 4, bytes_accessed=60000000, transcendentals=n_pair * seq * seq // 2),
        name="attn_fwd",
    )(me, cos_t, sin_t, bias_col, *slots)


def bwd_kernel(n_blk, coef, scale, me_ref, cos_ref, sin_ref, qkv_ref, out_ref, lse_ref, *refs):
    dctx = refs[:n_blk]
    dqkv_refs = refs[n_blk:2 * n_blk]
    db_ref = refs[2 * n_blk]
    k_nat, v_nat, do_t, delta, dq_acc, dk_acc, dv_acc, p_s, d_s = refs[2 * n_blk + 1:]
    me = me_ref[0]
    for s in range(n_blk):
        cols = pl.ds(pl.multiple_of(jnp.bitwise_xor(me, s) * BLK, BLK), BLK)
        d_rows = dctx[s][...]
        do_t[:, cols] = d_rows.astype(jnp.bfloat16)
        delta[:, cols] = jnp.sum(d_rows * out_ref[0, :, cols], axis=0, keepdims=True)
        k_nat[cols, :] = qkv_ref[0, K_ROWS, cols].T
        v_nat[cols, :] = qkv_ref[0, V_ROWS, cols].T
    clear(dq_acc, dk_acc, dv_acc)
    lanes_i = lax.broadcasted_iota(jnp.int32, (BK, SUB), 1) - lax.broadcasted_iota(jnp.int32, (BK, SUB), 0)

    def at(start, offset, size):
        return pl.ds(pl.multiple_of(start * BLK + offset, SUB), size)

    def stage1(k_blk, q_blk, r, c, diag):
        shift = c * SUB - r * BK
        k_len = min(BK, shift + SUB) if diag else BK
        q_sl = at(q_blk, c * SUB, SUB)
        k_sl = at(k_blk, r * BK, k_len)
        scores = nn_dot(k_nat[k_sl, :], qkv_ref[0, Q_ROWS, q_sl])
        d_probs = nn_dot(v_nat[k_sl, :], do_t[:, q_sl])
        probs = jnp.exp2(scores * coef - lse_ref[0, :, q_sl])
        if diag and shift < k_len:
            probs = jnp.where(lanes_i[:k_len] >= -shift, probs, 0.0)
        d_scores = (probs * (d_probs - delta[:, q_sl])).astype(jnp.bfloat16)
        rows, cols = slice(r * BK, r * BK + k_len), slice(c * SUB, (c + 1) * SUB)
        p_s[rows, cols] = probs.astype(jnp.bfloat16)
        d_s[rows, cols] = d_scores
        if k_len < BK:
            rest = slice(r * BK + k_len, (r + 1) * BK)
            p_s[rest, cols] = jnp.zeros((BK - k_len, SUB), jnp.bfloat16)
            d_s[rest, cols] = jnp.zeros((BK - k_len, SUB), jnp.bfloat16)

    def stage2(k_blk, q_blk, r, c):
        q_sl = at(q_blk, c * SUB, 2 * SUB)
        k_sl = at(k_blk, r * BK, BK)
        rows, cols = slice(r * BK, (r + 1) * BK), slice(c * SUB, (c + 2) * SUB)
        dv_acc[:, k_sl] += nt_dot(do_t[:, q_sl], p_s[rows, cols])
        dk_acc[:, k_sl] += nt_dot(qkv_ref[0, Q_ROWS, q_sl], d_s[rows, cols])
        dq_acc[:, q_sl] += nn_dot(qkv_ref[0, K_ROWS, k_sl], d_s[rows, cols])

    def body(k_blk, q_blk, diag):
        firsts = [(r, c) for r in range(BLK // BK) for c in range(BLK // SUB) if not diag or (c + 1) * SUB > r * BK]
        ready = []
        for r, c in firsts:
            stage1(k_blk, q_blk, r, c, diag)
            if ready:
                stage2(k_blk, q_blk, *ready.pop(0))
            if c % 2:
                ready.append((r, c - 1))
        for item in ready:
            stage2(k_blk, q_blk, *item)

    def one_k(k_blk, _):
        body(k_blk, k_blk, True)
        lax.fori_loop(k_blk + 1, n_blk, lambda q_blk, c: (body(k_blk, q_blk, False), c)[1], 0)
        return 0

    lax.fori_loop(0, n_blk, one_k, 0)
    lanes = jnp.zeros((TRIO, 128), jnp.float32)
    for s in range(n_blk):
        cols = pl.ds(pl.multiple_of(jnp.bitwise_xor(me, s) * BLK, BLK), BLK)
        cos_t, sin_t = cos_ref[:, cols], -sin_ref[:, cols]
        g = jnp.concatenate([turn(dq_acc[:, cols] * scale, cos_t, sin_t), turn(dk_acc[:, cols] * scale, cos_t, sin_t), dv_acc[:, cols]], axis=0)
        dqkv_refs[s][...] = g.astype(jnp.bfloat16)
        for c in range(BLK // 128):
            lanes += g[:, c * 128:(c + 1) * 128]
    db_ref[0] = lanes


def attn_bwd(me, cos_t, sin_t, qkv, outs, lse, dctx, coef, scale, h_from, h_cnt):
    n_blk = len(dctx)
    _, toks = dctx[0].shape
    batch, seq = toks // BLK, n_blk * BLK
    full = lambda h, b, me: (0, 0)
    hb_in = lambda h, b, me: (h + h_from, b)
    hb = lambda h, b, me: (h, b)
    one = lambda h, b, me: ((h + h_from) * batch + b, 0, 0)
    n_pair = h_cnt * batch
    return pl.pallas_call(
        lambda *refs: bwd_kernel(n_blk, coef, scale, *refs),
        grid_spec=pltpu.PrefetchScalarGridSpec(
            num_scalar_prefetch=1, grid=(h_cnt, batch),
            in_specs=[*[pl.BlockSpec((8, seq), full)] * 2, pl.BlockSpec((1, TRIO, seq), one), pl.BlockSpec((1, HD, seq), one), pl.BlockSpec((1, 1, seq), one)] + [pl.BlockSpec((HD, BLK), hb_in)] * n_blk,
            out_specs=[pl.BlockSpec((TRIO, BLK), hb)] * n_blk + [pl.BlockSpec((1, TRIO, 128), lambda h, b, me: (h * batch + b, 0, 0))],
            scratch_shapes=[pltpu.VMEM((seq, HD), jnp.bfloat16), pltpu.VMEM((seq, HD), jnp.bfloat16), pltpu.VMEM((HD, seq), jnp.bfloat16), pltpu.VMEM((1, seq), jnp.float32)] + [pltpu.VMEM((HD, seq), jnp.float32)] * 3 + [pltpu.VMEM((BLK, BLK), jnp.bfloat16)] * 2),
        out_shape=[jax.ShapeDtypeStruct((h_cnt * TRIO, toks), jnp.bfloat16)] * n_blk + [jax.ShapeDtypeStruct((n_pair, TRIO, 128), jnp.float32)],
        compiler_params=pltpu.CompilerParams(dimension_semantics=("arbitrary", "arbitrary"), vmem_limit_bytes=VMEM_GRANT),
        cost_estimate=pl.CostEstimate(flops=n_pair * seq * seq * 2 * HD * 10, bytes_accessed=80000000, transcendentals=n_pair * seq * seq // 2),
        name="attn_bwd",
    )(me, cos_t, sin_t, qkv, outs, lse, *dctx)


ERFC_P = 0.39
ERFC_C = (0.2353252191761132, 0.09138841398016789, 0.6495594000437396, -0.6354002804457791, 0.8866643709404932, -0.2275371253934527)
GELU_STEP = ERFC_P * 0.5 ** 0.5
TILE = 512
CHUNK = 512
STRIP = 16
PIECE = 256


def gelu_pair(pre):
    step = 1.0 / (1.0 + GELU_STEP * jnp.abs(pre))
    poly = 0.5 * ERFC_C[5]
    for coefficient in ERFC_C[4::-1]:
        poly = poly * step + 0.5 * coefficient
    bell = jnp.exp2(pre * pre * (-0.5 * LOG2E))
    tail = poly * step * bell
    cdf = jnp.where(pre >= 0.0, 1.0 - tail, tail)
    return pre * cdf, cdf + pre * bell * ((2.0 * 3.141592653589793) ** -0.5)


def clear(*refs):
    for ref in refs:
        ref[...] = jnp.zeros_like(ref)


def move(sems, *pairs):
    copies = [pltpu.make_async_copy(src, dst, sems.at[i]) for i, (src, dst) in enumerate(pairs)]
    for copy in copies:
        copy.start()
    for copy in copies:
        copy.wait()


def mlp_kernel(own, n_in, n_tile, core_ref, *refs):
    m_in, g_in = refs[:n_in], refs[n_in:2 * n_in]
    wu, wd, bu = refs[2 * n_in:2 * n_in + 3]
    refs = refs[2 * n_in + 3:]
    if own:
        dwu_out, dwd_out = refs[:2]
        mlp_out, dm_out, db_out = refs[2:2 + n_in], refs[2 + n_in:2 + 2 * n_in], refs[2 + 2 * n_in]
        refs = refs[3 + 2 * n_in:]
    else:
        dwu_in, dwd_in, dwu_full, dwd_full, dwu_out, dwd_out = refs[:6]
        refs = refs[6:]
    m_s, g_s, mt_s, a_s, d_s, at_s, acc_u, acc_d, u_s, v_s, db_s, sems = refs
    step = pl.program_id(0)
    last = n_in * n_tile - 1
    half = wu.shape[1]

    @pl.when(step == 0)
    def _():
        if own:
            clear(acc_u, acc_d, db_out)
        else:
            move(sems, (dwu_in, acc_u), (dwd_in, acc_d))

    for i in range(n_in):
        @pl.when(step // n_tile == i)
        def _(i=i):
            rows = m_in[i][...]
            m_s[...] = rows
            g_s[...] = g_in[i][...]
            mt_s[...] = rows.T

    n_chunk = half // CHUNK

    def first(f):
        def piece(c, is_up):
            inner = slice(c, c + PIECE)
            if is_up:
                u_s[f % 2, :, inner] = nn_dot(m_s[...], wu[:, f * CHUNK + c:f * CHUNK + c + PIECE])
            else:
                v_s[f % 2, :, inner] = nt_dot(g_s[...], wd[f * CHUNK + c:f * CHUNK + c + PIECE, :])

        return [functools.partial(piece, c, is_up) for c in range(0, CHUNK, PIECE) for is_up in (True, False)]

    def middle(f):
        cols = slice(f * CHUNK, (f + 1) * CHUNK)

        def strip(r):
            rows = slice(r, r + STRIP)
            act, slope = gelu_pair(u_s[f % 2, rows, :] + bu[:, cols])
            d_up = v_s[f % 2, rows, :] * slope
            a_s[rows, cols] = act.astype(jnp.bfloat16)
            d_s[rows, cols] = d_up.astype(jnp.bfloat16)
            if own:
                db_s[:, cols] += sum(d_up[q:q + 8] for q in range(0, STRIP, 8))

        return [functools.partial(strip, r) for r in range(0, TILE, STRIP)]

    def turned(f):
        cols = slice(f * CHUNK, (f + 1) * CHUNK)
        at_s[cols, :] = a_s[:, cols].T

    def second(f):
        cols = slice(f * CHUNK, (f + 1) * CHUNK)

        def down(c):
            acc_d[cols, c:c + PIECE] += nn_dot(at_s[cols, :], g_s[:, c:c + PIECE])

        def up(c, r):
            acc_u[r:r + TILE, f * CHUNK + c:f * CHUNK + c + PIECE] += nn_dot(mt_s[r:r + TILE, :], d_s[:, f * CHUNK + c:f * CHUNK + c + PIECE])

        width = m_s.shape[1]
        downs = [functools.partial(down, c) for c in range(0, width, PIECE)]
        return downs + [functools.partial(up, c, r) for r in range(0, width, TILE) for c in range(0, CHUNK, PIECE)]

    if own:
        clear(db_s)
    for t in range(n_chunk + 2):
        mxu = first(t) if t < n_chunk else []
        if t > 1:
            mxu = mxu + second(t - 2)
        vpu = middle(t - 1) if 0 < t <= n_chunk else []
        done = 0
        for i, piece in enumerate(mxu):
            piece()
            upto = len(vpu) * (i + 1) // len(mxu)
            for strip in vpu[done:upto]:
                strip()
            done = upto
        if vpu:
            turned(t - 1)
    if own:
        db_out[...] += jnp.sum(db_s[...], axis=0, keepdims=True)
    if own:
        for i in range(n_in):
            @pl.when(step // n_tile == i)
            def _(i=i):
                mlp_out[i][...] = nn_dot(a_s[...], wd[...])
                dm_out[i][...] = nt_dot(d_s[...], wu[...])

    @pl.when(step == last)
    def _():
        moves = [(acc_u, dwu_out), (acc_d, dwd_out)]
        if not own:
            mine = pl.ds(pl.multiple_of(core_ref[0] * half, half), half)
            moves += [(acc_u, dwu_full.at[:, mine]), (acc_d, dwd_full.at[mine, :])]
        move(sems, *moves)


def mlp_call(own, core, ms, gs, wu, wd, bu, dw=None):
    n_in = len(ms)
    toks, width = ms[0].shape
    half = wu.shape[1] // 2
    n_tile = toks // TILE

    def rows_of(i):
        return pl.BlockSpec((TILE, width), lambda t, core, i=i: (jnp.clip(t - i * n_tile, 0, n_tile - 1), 0))

    keep = lambda t, core: (0, 0)
    once = pl.Buffered(1)
    any_spec = pl.BlockSpec(memory_space=pl.ANY)
    in_specs = [rows_of(i) for i in range(n_in)] * 2 + [pl.BlockSpec((width, half), lambda t, core: (0, core[0]), pipeline_mode=once), pl.BlockSpec((half, width), lambda t, core: (core[0], 0), pipeline_mode=once), pl.BlockSpec((1, half), keep)]
    f32 = jnp.float32
    out_shape = [jax.ShapeDtypeStruct((width, half), f32), jax.ShapeDtypeStruct((half, width), f32)]
    out_specs = [any_spec, any_spec]
    args = [core] + list(ms) + list(gs) + [wu, wd, bu]
    if own:
        out_shape += [jax.ShapeDtypeStruct((toks, width), f32)] * (2 * n_in) + [jax.ShapeDtypeStruct((1, half), f32)]
        out_specs += [rows_of(i) for i in range(n_in)] * 2 + [pl.BlockSpec((1, half), keep)]
    else:
        in_specs += [any_spec, any_spec]
        args += list(dw)
        out_shape = [jax.ShapeDtypeStruct((width, 2 * half), f32), jax.ShapeDtypeStruct((2 * half, width), f32)] + out_shape
        out_specs = [any_spec, any_spec] + out_specs
    bf = jnp.bfloat16
    return pl.pallas_call(
        lambda *refs: mlp_kernel(own, n_in, n_tile, *refs),
        grid_spec=pltpu.PrefetchScalarGridSpec(num_scalar_prefetch=1, grid=(n_in * n_tile,), in_specs=in_specs, out_specs=out_specs, scratch_shapes=[pltpu.VMEM((TILE, width), bf), pltpu.VMEM((TILE, width), bf), pltpu.VMEM((width, TILE), bf), pltpu.VMEM((TILE, half), bf), pltpu.VMEM((TILE, half), bf), pltpu.VMEM((half, TILE), bf), pltpu.VMEM((width, half), f32), pltpu.VMEM((half, width), f32), pltpu.VMEM((2, TILE, CHUNK), f32), pltpu.VMEM((2, TILE, CHUNK), f32), pltpu.VMEM((8, half), f32), pltpu.SemaphoreType.DMA((4,))]),
        out_shape=out_shape,
        compiler_params=pltpu.CompilerParams(dimension_semantics=("arbitrary",), vmem_limit_bytes=66000000),
        cost_estimate=pl.CostEstimate(flops=n_in * toks * width * half * (12 if own else 8), bytes_accessed=80000000, transcendentals=n_in * toks * half * 2),
        name="mlp_own" if own else "mlp_far",
    )(*args)


def norm_rows(rows):
    mean = jnp.mean(rows, axis=-1, keepdims=True)
    centered = rows - mean
    inv_std = lax.rsqrt(jnp.mean(centered * centered, axis=-1, keepdims=True) + EPS)
    return centered * inv_std, inv_std


def prep_kernel(n_in, n_tile, me_ref, *refs):
    x_in = refs[:n_in]
    w_ref, vec_ref = refs[n_in:n_in + 2]
    outs = refs[n_in + 2:]
    for i in range(n_in):
        @pl.when(pl.program_id(0) // n_tile == i)
        def _(i=i):
            x_norm, _ = norm_rows(x_in[i][...].astype(jnp.float32))
            h_bf = (x_norm * vec_ref[0:1, :] + vec_ref[1:2, :]).astype(jnp.bfloat16)
            outs[3 * i][...] = h_bf
            outs[3 * i + 1][...] = (x_norm * vec_ref[2:3, :] + vec_ref[3:4, :]).astype(jnp.bfloat16)
            outs[3 * i + 2][...] = nt_dot(w_ref[...], h_bf)


def clip_rows(i, n_tile):
    return lambda t, me: (jnp.clip(t - i * n_tile, 0, n_tile - 1), 0)


def clip_cols(i, n_tile):
    return lambda t, me: (0, jnp.clip(t - i * n_tile, 0, n_tile - 1))


def prep_call(me, xs, w_t, vecs, q_rows):
    n_in = len(xs)
    toks, width = xs[0].shape
    n_tile = toks // TILE
    bf = jnp.bfloat16
    out_specs, out_shape = [], []
    for i in range(n_in):
        out_specs += [pl.BlockSpec((TILE, width), clip_rows(i, n_tile))] * 2 + [pl.BlockSpec((q_rows, TILE), clip_cols(i, n_tile))]
        out_shape += [jax.ShapeDtypeStruct((toks, width), bf)] * 2 + [jax.ShapeDtypeStruct((q_rows, toks), jnp.float32)]
    got = pl.pallas_call(
        lambda *refs: prep_kernel(n_in, n_tile, *refs),
        grid_spec=pltpu.PrefetchScalarGridSpec(
            num_scalar_prefetch=1, grid=(n_in * n_tile,),
            in_specs=[pl.BlockSpec((TILE, width), clip_rows(i, n_tile)) for i in range(n_in)] + [pl.BlockSpec((q_rows, width), lambda t, me: (me[0], 0)), pl.BlockSpec((4, width), lambda t, me: (0, 0))],
            out_specs=out_specs),
        out_shape=out_shape,
        compiler_params=pltpu.CompilerParams(dimension_semantics=("arbitrary",), vmem_limit_bytes=VMEM_GRANT),
        cost_estimate=pl.CostEstimate(flops=n_in * toks * width * q_rows * 2, bytes_accessed=n_in * 20000000, transcendentals=0),
        name="prep",
    )(me, *xs, w_t, vecs)
    return [got[3 * i:3 * i + 3] for i in range(n_in)]


def wgrad_kernel(n_slot, n_head, n_tile, *refs):
    dq = refs[:n_slot * n_head]
    h_in = refs[n_slot * n_head:n_slot * (n_head + 1)]
    ctx = refs[n_slot * (n_head + 1):n_slot * (n_head + 2)]
    g_in = refs[n_slot * (n_head + 2):n_slot * (n_head + 3)]
    w_out, o_out = refs[n_slot * (n_head + 3):]

    @pl.when(pl.program_id(0) == 0)
    def _():
        clear(w_out, o_out)

    for s in range(n_slot):
        @pl.when(pl.program_id(0) // n_tile == s)
        def _(s=s):
            lhs = jnp.concatenate([dq[s * n_head + hh][...] for hh in range(n_head)], axis=0)
            w_out[...] += nn_dot(lhs, h_in[s][...])
            o_out[...] += nn_dot(ctx[s][...], g_in[s][...])


def wgrad_call(dq, hs, ctx, gs):
    n_slot, n_head = len(dq), len(dq[0])
    toks, width = hs[0].shape
    n_tile = toks // TILE
    rows = TRIO

    def c_spec(s, r):
        return pl.BlockSpec((r, TILE), lambda t, s=s: (0, jnp.clip(t - s * n_tile, 0, n_tile - 1)))

    def r_spec(s):
        return pl.BlockSpec((TILE, width), lambda t, s=s: (jnp.clip(t - s * n_tile, 0, n_tile - 1), 0))

    keep = lambda t: (0, 0)
    sizes = (n_head * rows, n_head * HD)
    return pl.pallas_call(
        lambda *refs: wgrad_kernel(n_slot, n_head, n_tile, *refs),
        grid=(n_slot * n_tile,),
        in_specs=[c_spec(s, rows) for s in range(n_slot) for _ in range(n_head)] + [r_spec(s) for s in range(n_slot)] + [c_spec(s, n_head * HD) for s in range(n_slot)] + [r_spec(s) for s in range(n_slot)],
        out_specs=[pl.BlockSpec((r, width), keep) for r in sizes],
        out_shape=[jax.ShapeDtypeStruct((r, width), jnp.float32) for r in sizes],
        compiler_params=pltpu.CompilerParams(dimension_semantics=("arbitrary",), vmem_limit_bytes=VMEM_GRANT),
        cost_estimate=pl.CostEstimate(flops=n_slot * toks * width * sum(sizes) * 2, bytes_accessed=60000000, transcendentals=0),
        name="wgrad",
    )(*[p for part in dq for p in part], *hs, *ctx, *gs)


FIN = 256


def finish_kernel(n_slot, n_head, me_ref, x_ref, dy_ref, ma_ref, mb_ref, da_ref, db_ref, w_ref, wo_ref, vec_ref, *refs):
    dq = refs[:n_slot * n_head]
    ctx = refs[n_slot * n_head:n_slot * (n_head + 1)]
    y_out, dx_out, sums = refs[n_slot * (n_head + 1):]
    me = me_ref[0]
    width = x_ref.shape[1]
    d_h = jnp.zeros((FIN, width), jnp.float32)
    proj = jnp.zeros((FIN, width), jnp.float32)
    for s in range(n_slot):
        owner = jnp.bitwise_xor(me, s)
        lhs = jnp.concatenate([dq[s * n_head + hh][...] for hh in range(n_head)], axis=0)
        q_rows = n_head * TRIO
        d_h += nn_dot(lhs.T, w_ref[pl.ds(pl.multiple_of(owner * q_rows, q_rows), q_rows), :])
        c_rows = n_head * HD
        proj += nn_dot(ctx[s][...].T, wo_ref[pl.ds(pl.multiple_of(owner * c_rows, c_rows), c_rows), :])
    rows = x_ref[...].astype(jnp.float32)
    y_out[...] = (rows + (proj + vec_ref[2:3, :]) + (ma_ref[...] + mb_ref[...] + vec_ref[3:4, :])).astype(jnp.bfloat16)
    x_norm, inv_std = norm_rows(rows)
    d_m = da_ref[...] + db_ref[...]
    d_norm = d_h * vec_ref[0:1, :] + d_m * vec_ref[1:2, :]
    d_rows = inv_std * (d_norm - jnp.mean(d_norm, axis=-1, keepdims=True) - x_norm * jnp.mean(d_norm * x_norm, axis=-1, keepdims=True))
    dy = dy_ref[...]
    dx_out[...] = dy + d_rows

    @pl.when(pl.program_id(0) == 0)
    def _():
        clear(sums)

    for i, part in enumerate((d_h * x_norm, d_h, d_m * x_norm, d_m, dy)):
        sums[i:i + 1, :] += jnp.sum(part, axis=0, keepdims=True)


def finish_call(me, x0, dy, ma, mb, da, db, w_t, w_out, vecs, dq, ctx):
    n_slot, n_head = len(dq), len(dq[0])
    toks, width = x0.shape
    row = lambda t, me: (t, 0)
    col = lambda t, me: (0, t)
    keep = lambda t, me: (0, 0)
    once = pl.Buffered(1)
    return pl.pallas_call(
        lambda *refs: finish_kernel(n_slot, n_head, *refs),
        grid_spec=pltpu.PrefetchScalarGridSpec(
            num_scalar_prefetch=1, grid=(toks // FIN,),
            in_specs=[pl.BlockSpec((FIN, width), row)] * 6 + [pl.BlockSpec(w_t.shape, keep, pipeline_mode=once), pl.BlockSpec(w_out.shape, keep, pipeline_mode=once), pl.BlockSpec((4, width), keep)] + [pl.BlockSpec((TRIO, FIN), col)] * (n_slot * n_head) + [pl.BlockSpec((n_head * HD, FIN), col)] * n_slot,
            out_specs=[pl.BlockSpec((FIN, width), row), pl.BlockSpec((FIN, width), row), pl.BlockSpec((8, width), keep)]),
        out_shape=[jax.ShapeDtypeStruct((toks, width), jnp.bfloat16), jax.ShapeDtypeStruct((toks, width), jnp.float32), jax.ShapeDtypeStruct((8, width), jnp.float32)],
        compiler_params=pltpu.CompilerParams(dimension_semantics=("arbitrary",), vmem_limit_bytes=VMEM_GRANT),
        cost_estimate=pl.CostEstimate(flops=toks * width * n_head * n_slot * 4 * HD * 2, bytes_accessed=80000000, transcendentals=0),
        name="finish",
    )(me, x0, dy, ma, mb, da, db, w_t, w_out, vecs, *[p for part in dq for p in part], *ctx)


def dot32(spec, lhs, rhs):
    return jnp.einsum(spec, lhs, rhs, preferred_element_type=jnp.float32)


def solution(mesh):
    n_cp = mesh.shape['cp']
    row_spec = P('dp', 'cp')
    in_specs = (row_spec, row_spec) + (P(),) * 12
    out_specs = (row_spec, row_spec, P('dp'), P('dp'), P('dp'), P('dp'), P('dp'), P('dp'), P('dp'), P('dp'), P('dp'), P('dp'), P('dp'), P('dp'))

    def swap(value, mask):
        return lax.ppermute(value, 'cp', [(i, i ^ mask) for i in range(n_cp)])

    def layer_body(x_blk, dy_blk, ln1_gain, ln1_bias, ln2_gain, ln2_bias, w_qkv, b_qkv, w_out, b_out, w_up, b_up, w_down, b_down):
        batch, row_count, width = x_blk.shape
        heads, hd = w_qkv.shape[1], w_qkv.shape[3]
        ff = w_up.shape[1]
        toks, seq = batch * row_count, n_cp * row_count
        my_heads = heads // n_cp
        q_rows = my_heads * 3 * hd
        c_rows = my_heads * hd
        half = ff // 2
        scale = hd ** -0.5
        coef = scale * LOG2E
        me = lax.axis_index('cp')
        core = me % 2
        slot_of = [jnp.bitwise_xor(me, s) for s in range(n_cp)]
        bf, f32 = jnp.bfloat16, jnp.float32
        me_arr = me.astype(jnp.int32).reshape(1)

        x0 = x_blk.reshape(toks, width)
        dy32 = dy_blk.reshape(toks, width)
        x2 = swap(x0, 2)
        x1 = swap(x0, 1)
        g0 = dy32.astype(bf)
        g1 = swap(g0, 1)
        g2 = swap(g0, 2)

        w_t = jnp.transpose(w_qkv, (1, 2, 3, 0)).reshape(heads * 3 * hd, width)
        w_o_mine = lax.dynamic_slice_in_dim(w_out, me * c_rows, c_rows, 0)
        bias_col = lax.dynamic_slice_in_dim(b_qkv.astype(f32).reshape(heads * 3 * hd, 1), me * q_rows, q_rows, 0)
        inv_freq = ROPE_BASE ** (-2.0 * jnp.arange(8, dtype=f32) / 16)
        angles = inv_freq[:, None] * jnp.arange(seq, dtype=f32)[None, :]
        cos_t, sin_t = jnp.cos(angles), jnp.sin(angles)
        vecs = jnp.stack([ln1_gain, ln1_bias, ln2_gain, ln2_bias])
        b_up_h = lax.dynamic_slice_in_dim(b_up, core * half, half, 0).astype(f32).reshape(1, half)
        core_arr = jnp.stack([core.astype(jnp.int32), jnp.int32(1)])

        near = prep_call(me_arr, [x0, x1], w_t, vecs, q_rows)
        dwu, dwd, mlp_0, mlp_1, dm_0, dm_1, db_up_h = mlp_call(True, core_arr, [near[0][1], near[1][1]], [g0, g1], w_up, w_down, b_up_h)
        x2, dwu = lax.optimization_barrier((x2, dwu))
        x3 = swap(x2, 1)
        far = prep_call(me_arr, [x2, x3], w_t, vecs, q_rows)
        mlp_b, dm_b = swap(mlp_1, 1), swap(dm_1, 1)
        h_in = [p[0] for p in near + far]
        fwd = attn_fwd(me_arr, cos_t, sin_t, bias_col, [p[2] for p in near + far], coef)
        qkv, outs, lse, ctx = fwd[0], fwd[1], fwd[2], fwd[3:]
        ctx_got = [ctx[0]] + [swap(ctx[s], s) for s in range(1, n_cp)]

        g2, outs = lax.optimization_barrier((g2, outs))
        g3 = swap(g2, 1)
        gs = [g0, g1, g2, g3]
        dctx = [dot32('ce,te->ct', w_o_mine, gs[s]) for s in range(n_cp)]
        dq_parts, db_parts = [], []
        for hh in range(my_heads):
            got = attn_bwd(me_arr, cos_t, sin_t, qkv, outs, lse, dctx, coef, scale, hh, 1)
            dq_parts.append(got[:n_cp])
            db_parts.append(jnp.sum(got[n_cp], axis=(0, 2)))
        dq_mine = [[dq_parts[hh][s] for hh in range(my_heads)] for s in range(n_cp)]
        dq_got = [dq_mine[0]] + [[swap(part, s) for part in dq_mine[s]] for s in range(1, n_cp)]
        d_w_t, d_w_o = wgrad_call(dq_mine, h_in, ctx, gs)

        far_m, d_w_o, d_w_t = lax.optimization_barrier(([p[1] for p in far], d_w_o, d_w_t))
        dwu_full, dwd_full, dwu_h, dwd_h = mlp_call(False, core_arr, far_m, [g2, g3], w_up, w_down, b_up_h, (dwu, dwd))

        def collect(mine):
            far_part = swap(mine, 2)
            near_part, diag = swap(mine, 1), swap(far_part, 1)
            rows = mine.shape[0]
            full = jnp.zeros((n_cp * rows,) + mine.shape[1:], mine.dtype)
            for s, part in enumerate((mine, near_part, far_part, diag)):
                full = lax.dynamic_update_slice_in_dim(full, part, slot_of[s] * rows, 0)
            return full

        d_w_out = collect(d_w_o)
        d_w_qkv = jnp.transpose(collect(d_w_t).reshape(heads, 3, hd, width), (3, 0, 1, 2))

        x0f, dwu_h, dwd_h = lax.optimization_barrier((x0, dwu_h, dwd_h))
        fin_vecs = jnp.stack([ln1_gain, ln2_gain, b_out.astype(f32), b_down.astype(f32)])
        y_rows, dx, sums = finish_call(me_arr, x0f, dy32, mlp_0, mlp_b, dm_0, dm_b, w_t, w_out, fin_vecs, dq_got, ctx_got)
        d_w_up = lax.dynamic_update_slice_in_dim(dwu_full, swap(dwu_h, 1), (1 - core) * half, 1)
        d_w_down = lax.dynamic_update_slice_in_dim(dwd_full, swap(dwd_h, 1), (1 - core) * half, 0)

        db_qkv = lax.dynamic_update_slice_in_dim(jnp.zeros((heads * 3 * hd,), f32), jnp.concatenate(db_parts), me * q_rows, 0)
        db_up = lax.dynamic_update_slice_in_dim(jnp.zeros((ff,), f32), db_up_h.reshape(half), core * half, 0)
        small = lax.psum(jnp.concatenate([sums[:5].reshape(5 * width), db_qkv, db_up]), 'cp')
        cut = [width, 2 * width, 3 * width, 4 * width, 5 * width, 5 * width + heads * 3 * hd]
        s_g1, s_b1, s_g2, s_b2, s_dy, s_bq, s_bu = jnp.split(small, cut)
        return (y_rows.reshape(x_blk.shape), dx.reshape(dy_blk.shape), s_g1, s_b1, s_g2, s_b2, d_w_qkv, s_bq.reshape(heads, 3, hd), d_w_out, s_dy, d_w_up, s_bu, d_w_down, s_dy)


    return jax.shard_map(layer_body, mesh=mesh, in_specs=in_specs, out_specs=out_specs, check_vma=False)
```

time: 1430 us -> 1030 us (0.72)
  matrix products: 703 us -> 19.3 us
  Pallas kernels: 412 us -> 705 us
  waiting for transfers between devices: 145 us -> 212 us
  other arithmetic: 56.7 us -> 12.6 us
  local copies, waits for them, and re-layouts: 67 us -> 52 us
    dot_general x43 -> x4, matrix products: 703 us -> 19.3 us  [dot32(): return jnp.einsum(spec, lhs, rhs, preferred_element_type=jnp.float32)]
    pallas_call x0 -> x6, Pallas kernels: none -> 373 us  [the longest x2 268 us: mlp_call(): pl.pallas_call(lambda *refs: mlp_kernel(own, n_in, n_tile, *refs), grid_s...]
    pallas_call x4, Pallas kernels: 296 us -> 216 us  [attn_bwd(): pl.pallas_call(lambda *refs: bwd_kernel(n_blk, coef, scale, *refs), grid_...]
    ppermute x31, waiting for transfers between devices: 145 us -> 212 us  [swap(): return lax.ppermute(value, 'cp', [(i, i ^ mask) for i in range(n_cp)])]
    reduce_sum x13 -> x4, other arithmetic: 29.2 us -> 3.24 us  [layer_body(): db_parts.append(jnp.sum(got[n_cp], axis=(0, 2)))]
    broadcast_in_dim x4 -> x2, local copies, waits for them, and re-layouts: 17.5 us -> 0.01 us  [the longest x1 0.01 us: layer_body(): jnp.zeros((heads * 3 * hd,), f32)]
    add x1 -> x0, other arithmetic: 14.7 us -> none  [local_layer(): dx = dy32 + dx1 + dx2]
  transfers between devices with their start and end apart: 31 -> 31, of which waited for: 6 -> 11; matrix products, arithmetic and copies ran while one was open for 57% -> 7% of each run, Pallas kernels for 29% -> 68%
where the time goes in v2:
time: 1030 us
  Pallas kernels  705 us (68%)
  waiting for transfers between devices  212 us (21%)
  local copies, waits for them, and re-layouts  52 us (5%)
  matrix products  19.3 us (2%)
  starting transfers between devices  16.4 us (2%)
  other arithmetic  12.6 us (1%)
  blocking collectives  11 us (1%)
    pallas_call x2, Pallas kernels, mlp_call(): pl.pallas_call(lambda *refs: mlp_kernel(own, n_in, n_tile, *refs), grid_s...  268 us
    pallas_call x4, Pallas kernels, attn_bwd(): pl.pallas_call(lambda *refs: bwd_kernel(n_blk, coef, scale, *refs), grid_...  216 us
    ppermute x31, waiting for transfers between devices, swap(): return lax.ppermute(value, 'cp', [(i, i ^ mask) for i in range(n_cp)])  212 us
    pallas_call x1, Pallas kernels, attn_fwd(): pl.pallas_call(lambda *refs: fwd_kernel(n_blk, coef, *refs), grid_spec=pl...  116 us
    pallas_call x2, Pallas kernels, prep_call(): pl.pallas_call(lambda *refs: prep_kernel(n_in, n_tile, *refs), grid_spec=...  39 us
    pallas_call x1, Pallas kernels, finish_call(): pl.pallas_call(lambda *refs: finish_kernel(n_slot, n_head, *refs), grid_s...  33.6 us
    pallas_call x1, Pallas kernels, wgrad_call(): pl.pallas_call(lambda *refs: wgrad_kernel(n_slot, n_head, n_tile, *refs),...  32.6 us
  transfers between devices with their start and end apart: 31, of which 11 were waited for; matrix products, arithmetic and copies ran while one was open for 7% of the time, Pallas kernels for 68%

profile of v2, /device:TPU:0, one launch (start us, length us, event | category | flops | bytes accessed | tf_op | source)
XLA Modules:
  0.0 1029.9 jit_solution(1433489804732165642)
XLA Ops:
  1.6 6.1 bitcast_convert_fusion.refs_3_.refs_24_
  12.6 19.5 %prep.2 = (bf16[2048,1024]{1,0:T(8,128)(2,1)}, bf16[2048,1024]{1,0:T(8,128)(2,1)}, f32[768,2048]{1,0:T(8,128)}, bf16[2048,1024]{1,0:T(8,128)(2,1)}, bf16[2048,1024]{1,0:T(8,128)(2,1)}, /*index=5*/f32[768,2048]{1,0:T(8,128)}) custom-call(s32[1]{0:T(128)} %bitcast.refs_0_, bf16[2048,1024]{1,0:T(8,128)(2,1)} %bitcast.1.refs_1_, ...), custom_call_target="tpu_custom_call" | custom-call | flops 6442450944 | bytes 40000000 | tf_op jit(solution)/shard_map/prep/pallas_call | solution.py:468
  32.1 151.6 %mlp_own.1 = (f32[1024,2048]{1,0:T(8,128)}, f32[2048,1024]{1,0:T(8,128)}, f32[2048,1024]{1,0:T(8,128)}, f32[2048,1024]{1,0:T(8,128)}, f32[2048,1024]{1,0:T(8,128...) custom-call(s32[2]{0:T(128)} %pad_add_fusion.refs_0_, bf16[2048,1024]{1,0:T(8,128)(2,1)} %get-tuple-element.80.refs_1_, ...), custom_call_target="tpu_custom_call" | custom-call | flops 103079215104 | bytes 80000000 | tf_op jit(solution)/shard_map/mlp_own/pallas_call | solution.py:420
  191.3 19.5 %prep.3 = (bf16[2048,1024]{1,0:T(8,128)(2,1)}, bf16[2048,1024]{1,0:T(8,128)(2,1)}, f32[768,2048]{1,0:T(8,128)}, bf16[2048,1024]{1,0:T(8,128)(2,1)}, bf16[2048,1024]{1,0:T(8,128)(2,1)}, /*index=5*/f32[768,2048]{1,0:T(8,128)}) custom-call(s32[1]{0:T(128)} %bitcast.refs_0_, bf16[2048,1024]{1,0:T(8,128)(2,1)} %collective-permute-done.refs_1_, ...), custom_call_target="tpu_custom_call" | custom-call | flops 6442450944 | bytes 40000000 | tf_op jit(solution)/shard_map/prep/pallas_call | solution.py:468
  210.7 116.2 %attn_fwd.1 = (bf16[8,192,4096]{2,1,0:T(8,128)(2,1)}, f32[8,64,4096]{2,1,0:T(8,128)}, f32[8,1,4096]{2,1,0:T(1,128)}, bf16[256,2048]{1,0:T(8,128)(2,1)}, bf16[256...) custom-call(s32[1]{0:T(128)} %bitcast.refs_0_, f32[8,4096]{1,0:T(8,128)} %get-tuple-element.168.refs_1_, ...), custom_call_target="tpu_custom_call" | custom-call | flops 68719476736 | bytes 60000000 | tf_op jit(solution)/shard_map/attn_fwd/pallas_call | solution.py:141
  348.7 53.8 %attn_bwd.7 = (bf16[192,2048]{1,0:T(8,128)(2,1)}, bf16[192,2048]{1,0:T(8,128)(2,1)}, bf16[192,2048]{1,0:T(8,128)(2,1)}, bf16[192,2048]{1,0:T(8,128)(2,1)}, f32[2,192,128]{2,1,0:T(8,128)}) custom-call(s32[1]{0:T(128)} %bitcast.refs_0_, f32[8,4096]{1,0:T(8,128)} %get-tuple-element.168.refs_1_, f32[8,4096]{1,0:T(8,128)} %get-tuple-element.167.refs_2_, ...), custom_call_target="tpu_custom_call" | custom-call | flops 42949672960 | bytes 80000000 | tf_op jit(solution)/shard_map/attn_bwd/pallas_call | solution.py:239
  402.6 54.0 %attn_bwd.6 = (bf16[192,2048]{1,0:T(8,128)(2,1)}, bf16[192,2048]{1,0:T(8,128)(2,1)}, bf16[192,2048]{1,0:T(8,128)(2,1)}, bf16[192,2048]{1,0:T(8,128)(2,1)}, f32[2,192,128]{2,1,0:T(8,128)}) custom-call(s32[1]{0:T(128)} %bitcast.refs_0_, f32[8,4096]{1,0:T(8,128)} %get-tuple-element.168.refs_1_, f32[8,4096]{1,0:T(8,128)} %get-tuple-element.167.refs_2_, ...), custom_call_target="tpu_custom_call" | custom-call | flops 42949672960 | bytes 80000000 | tf_op jit(solution)/shard_map/attn_bwd/pallas_call | solution.py:239
  456.6 53.9 %attn_bwd.5 = (bf16[192,2048]{1,0:T(8,128)(2,1)}, bf16[192,2048]{1,0:T(8,128)(2,1)}, bf16[192,2048]{1,0:T(8,128)(2,1)}, bf16[192,2048]{1,0:T(8,128)(2,1)}, f32[2,192,128]{2,1,0:T(8,128)}) custom-call(s32[1]{0:T(128)} %bitcast.refs_0_, f32[8,4096]{1,0:T(8,128)} %get-tuple-element.168.refs_1_, f32[8,4096]{1,0:T(8,128)} %get-tuple-element.167.refs_2_, ...), custom_call_target="tpu_custom_call" | custom-call | flops 42949672960 | bytes 80000000 | tf_op jit(solution)/shard_map/attn_bwd/pallas_call | solution.py:239
  510.4 54.2 %attn_bwd.4 = (bf16[192,2048]{1,0:T(8,128)(2,1)}, bf16[192,2048]{1,0:T(8,128)(2,1)}, bf16[192,2048]{1,0:T(8,128)(2,1)}, bf16[192,2048]{1,0:T(8,128)(2,1)}, f32[2,192,128]{2,1,0:T(8,128)}) custom-call(s32[1]{0:T(128)} %bitcast.refs_0_, f32[8,4096]{1,0:T(8,128)} %get-tuple-element.168.refs_1_, f32[8,4096]{1,0:T(8,128)} %get-tuple-element.167.refs_2_, ...), custom_call_target="tpu_custom_call" | custom-call | flops 42949672960 | bytes 80000000 | tf_op jit(solution)/shard_map/attn_bwd/pallas_call | solution.py:239
  564.6 32.6 %wgrad.1 = (f32[768,1024]{1,0:T(8,128)}, f32[256,1024]{1,0:T(8,128)}) custom-call(bf16[192,2048]{1,0:T(8,128)(2,1)} %get-tuple-element.95.refs_0_.refs_10_, bf16[192,2048]{1,0:T(8,128)(2,1)} %get-tuple-element.96.refs_1_.refs_11_, bf16[192,2048]{1,0:T(8,128)(2,1)} %get-tuple-element.97.refs_2_.refs_12_, ...), custom_call_target="tpu_custom_call" | custom-call | flops 17179869184 | bytes 60000000 | tf_op jit(solution)/shard_map/wgrad/pallas_call | solution.py:515
  597.9 116.3 %mlp_far.1 = (f32[1024,4096]{1,0:T(8,128)}, f32[4096,1024]{1,0:T(8,128)}, f32[1024,2048]{1,0:T(8,128)}, f32[2048,1024]{1,0:T(8,128)}) custom-call(s32[2]{0:T(128)} %pad_add_fusion.refs_0_, bf16[2048,1024]{1,0:T(8,128)(2,1)} %get-tuple-element.121.refs_1_, bf16[2048,1024]{1,0:T(8,128)(2,1)} %get-tuple-element.122.refs_2_, ...), custom_call_target="tpu_custom_call" | custom-call | flops 68719476736 | bytes 80000000 | tf_op jit(solution)/shard_map/mlp_far/pallas_call | solution.py:420
  716.7 18.3 %collective-permute-done.15.refs_21_ = bf16[192,2048]{1,0:T(8,128)(2,1)S(1)} collective-permute-done((bf16[192,2048]{1,0:T(8,128)(2,1)}, bf16[192,2048]{1,0:T(8,128)(2,1)S(1)}, u32[]{:S(2)}, u32[]{:S(2)}) %collective-permute-start.15) | collective-permute-done | bytes 786464 | tf_op jit(solution)/shard_map/ppermute | solution.py:593
  735.3 15.5 %collective-permute-done.19.refs_25_ = bf16[192,2048]{1,0:T(8,128)(2,1)S(1)} collective-permute-done((bf16[192,2048]{1,0:T(8,128)(2,1)}, bf16[192,2048]{1,0:T(8,128)(2,1)S(1)}, u32[]{:S(2)}, u32[]{:S(2)}) %collective-permute-start.19) | collective-permute-done | bytes 786464 | tf_op jit(solution)/shard_map/ppermute | solution.py:593
  753.3 15.4 %collective-permute-done.14.refs_20_ = bf16[192,2048]{1,0:T(8,128)(2,1)S(1)} collective-permute-done((bf16[192,2048]{1,0:T(8,128)(2,1)}, bf16[192,2048]{1,0:T(8,128)(2,1)S(1)}, u32[]{:S(2)}, u32[]{:S(2)}) %collective-permute-start.14) | collective-permute-done | bytes 786464 | tf_op jit(solution)/shard_map/ppermute | solution.py:593
  769.0 15.5 %collective-permute-done.18.refs_24_ = bf16[192,2048]{1,0:T(8,128)(2,1)S(1)} collective-permute-done((bf16[192,2048]{1,0:T(8,128)(2,1)}, bf16[192,2048]{1,0:T(8,128)(2,1)S(1)}, u32[]{:S(2)}, u32[]{:S(2)}) %collective-permute-start.18) | collective-permute-done | bytes 786464 | tf_op jit(solution)/shard_map/ppermute | solution.py:593
  785.3 17.1 %collective-permute-done.13.refs_19_ = bf16[192,2048]{1,0:T(8,128)(2,1)S(1)} collective-permute-done((bf16[192,2048]{1,0:T(8,128)(2,1)}, bf16[192,2048]{1,0:T(8,128)(2,1)S(1)}, u32[]{:S(2)}, u32[]{:S(2)}) %collective-permute-start.13) | collective-permute-done | bytes 786464 | tf_op jit(solution)/shard_map/ppermute | solution.py:593
  802.4 83.3 %collective-permute-done.17.refs_23_ = bf16[192,2048]{1,0:T(8,128)(2,1)S(1)} collective-permute-done((bf16[192,2048]{1,0:T(8,128)(2,1)}, bf16[192,2048]{1,0:T(8,128)(2,1)S(1)}, u32[]{:S(2)}, u32[]{:S(2)}) %collective-permute-start.17) | collective-permute-done | bytes 786464 | tf_op jit(solution)/shard_map/ppermute | solution.py:593
  887.3 18.9 %collective-permute-done.12.refs_18_ = bf16[192,2048]{1,0:T(8,128)(2,1)S(1)} collective-permute-done((bf16[192,2048]{1,0:T(8,128)(2,1)}, bf16[192,2048]{1,0:T(8,128)(2,1)S(1)}, u32[]{:S(2)}, u32[]{:S(2)}) %collective-permute-start.12) | collective-permute-done | bytes 786464 | tf_op jit(solution)/shard_map/ppermute | solution.py:593
  906.3 15.6 %collective-permute-done.16.refs_22_ = bf16[192,2048]{1,0:T(8,128)(2,1)S(1)} collective-permute-done((bf16[192,2048]{1,0:T(8,128)(2,1)}, bf16[192,2048]{1,0:T(8,128)(2,1)S(1)}, u32[]{:S(2)}, u32[]{:S(2)}) %collective-permute-start.16) | collective-permute-done | bytes 786464 | tf_op jit(solution)/shard_map/ppermute | solution.py:593
  932.7 6.4 broadcast_in_dim.16
  940.9 6.7 collective-permute-done.27
  947.6 33.6 %finish.1 = (bf16[2048,1024]{1,0:T(8,128)(2,1)}, f32[2048,1024]{1,0:T(8,128)}, f32[8,1024]{1,0:T(8,128)}) custom-call(s32[1]{0:T(128)} %bitcast.refs_0_, bf16[2048,1024]{1,0:T(8,128)(2,1)} %bitcast.1.refs_1_, f32[2048,1024]{1,0:T(8,128)} %bitcast.26, f32[2048,1024]{1,0:T(8,128)} %get-tuple-element.128.refs_3_, f32[2048,1024]{1,0:T(8,128)} %collective-permute-done.6.refs_4_, ...), custom_call_target="tpu_custom_call" | custom-call | flops 17179869184 | bytes 80000000 | tf_op jit(solution)/shard_map/finish/pallas_call | solution.py:569
  982.0 11.0 %psum.7 = f32[12288]{0:T(1024)S(1)} all-reduce(f32[12288]{0:T(1024)S(1)} %pad_maximum_fusion), channel_id=1, replica_groups=mesh['dp'=2,'cp'=4] {'cp'}, use_global_device_ids=true, to_apply=%region_4.5 | all-reduce | flops 12288 | bytes 98304 | tf_op jit(solution)/shard_map/psum | solution.py:677
  1010.4 8.6 constant_dynamic-update-slice_fusion
  (156 shorter events, 85.2 us)
Async XLA Ops:
  7.7 24.4 %collective-permute-start.2 = (bf16[2048,1024]{1,0:T(8,128)(2,1)}, bf16[2048,1024]{1,0:T(8,128)(2,1)}, u32[]{:S(2)}, u32[]{:S(2)}) collective-permute-start(bf16[2048,1024]{1,0:T(8,128)(2,1)} %bitcast_convert_fusion.refs_3_.refs_24_), channel_id=1, source_target_pairs={{0,1},{1,0},{2,3},{3,2},{4,5},{5,4},{6,7},{7,6}} | collective-permute-start | bytes 12582920 | tf_op jit(solution)/shard_map/ppermute | solution.py:593
  7.7 176.0 %collective-permute-start = (bf16[2048,1024]{1,0:T(8,128)(2,1)}, bf16[2048,1024]{1,0:T(8,128)(2,1)}, u32[]{:S(2)}, u32[]{:S(2)}) collective-permute-start(bf16[2048,1024]{1,0:T(8,128)(2,1)} %bitcast.1.refs_1_), channel_id=1, source_target_pairs={{0,2},{1,3},{2,0},{3,1},{4,6},{5,7},{6,4},{7,5}} | collective-permute-start | bytes 12582920 | tf_op jit(solution)/shard_map/ppermute | solution.py:593
  183.8 143.2 %collective-permute-start.4 = (bf16[2048,1024]{1,0:T(8,128)(2,1)}, bf16[2048,1024]{1,0:T(8,128)(2,1)}, u32[]{:S(2)}, u32[]{:S(2)}) collective-permute-start(bf16[2048,1024]{1,0:T(8,128)(2,1)} %bitcast_convert_fusion.refs_3_.refs_24_), channel_id=1, source_target_pairs={{0,2},{1,3},{2,0},{3,1},{4,6},{5,7},{6,4},{7,5}} | collective-permute-start | bytes 12582920 | tf_op jit(solution)/shard_map/ppermute | solution.py:593
  331.9 382.8 %collective-permute-start.6 = (f32[2048,1024]{1,0:T(8,128)}, f32[2048,1024]{1,0:T(8,128)}, u32[]{:S(2)}, u32[]{:S(2)}) collective-permute-start(f32[2048,1024]{1,0:T(8,128)} %get-tuple-element.129), channel_id=1, source_target_pairs={{0,1},{1,0},{2,3},{3,2},{4,5},{5,4},{6,7},{7,6}} | collective-permute-start | bytes 25165832 | tf_op jit(solution)/shard_map/ppermute | solution.py:593
  332.3 383.9 %collective-permute-start.7 = (f32[2048,1024]{1,0:T(8,128)}, f32[2048,1024]{1,0:T(8,128)}, u32[]{:S(2)}, u32[]{:S(2)}) collective-permute-start(f32[2048,1024]{1,0:T(8,128)} %get-tuple-element.131), channel_id=1, source_target_pairs={{0,1},{1,0},{2,3},{3,2},{4,5},{5,4},{6,7},{7,6}} | collective-permute-start | bytes 25165832 | tf_op jit(solution)/shard_map/ppermute | solution.py:593
  337.2 260.0 %collective-permute-start.20 = (bf16[256,2048]{1,0:T(8,128)(2,1)}, bf16[256,2048]{1,0:T(8,128)(2,1)}, u32[]{:S(2)}, u32[]{:S(2)}) collective-permute-start(bf16[256,2048]{1,0:T(8,128)(2,1)} %get-tuple-element.116.refs_21_), channel_id=1, source_target_pairs={{0,1},{1,0},{2,3},{3,2},{4,5},{5,4},{6,7},{7,6}} | collective-permute-start | bytes 3145736 | tf_op jit(solution)/shard_map/ppermute | solution.py:593
  337.6 376.6 %collective-permute-start.21 = (bf16[256,2048]{1,0:T(8,128)(2,1)}, bf16[256,2048]{1,0:T(8,128)(2,1)}, u32[]{:S(2)}, u32[]{:S(2)}) collective-permute-start(bf16[256,2048]{1,0:T(8,128)(2,1)} %get-tuple-element.117.refs_22_), channel_id=1, source_target_pairs={{0,2},{1,3},{2,0},{3,1},{4,6},{5,7},{6,4},{7,5}} | collective-permute-start | bytes 3145736 | tf_op jit(solution)/shard_map/ppermute | solution.py:593
  342.5 371.9 %collective-permute-start.22 = (bf16[256,2048]{1,0:T(8,128)(2,1)}, bf16[256,2048]{1,0:T(8,128)(2,1)}, u32[]{:S(2)}, u32[]{:S(2)}) collective-permute-start(bf16[256,2048]{1,0:T(8,128)(2,1)} %get-tuple-element.118.refs_23_), channel_id=1, source_target_pairs={{0,3},{1,2},{2,1},{3,0},{4,7},{5,6},{6,5},{7,4}} | collective-permute-start | bytes 3145736 | tf_op jit(solution)/shard_map/ppermute | solution.py:593
  597.2 119.2 %collective-permute-start.11 = (bf16[192,2048]{1,0:T(8,128)(2,1)}, bf16[192,2048]{1,0:T(8,128)(2,1)S(1)}, u32[]{:S(2)}, u32[]{:S(2)}) collective-permute-start(bf16[192,2048]{1,0:T(8,128)(2,1)} %get-tuple-element.102.refs_7_), channel_id=1, source_target_pairs={{0,1},{1,0},{2,3},{3,2},{4,5},{5,4},{6,7},{7,6}} | collective-permute-start | bytes 2359304 | tf_op jit(solution)/shard_map/ppermute | solution.py:593
  714.3 296.2 %collective-permute-start.30 = (f32[2048,1024]{1,0:T(8,128)}, f32[2048,1024]{1,0:T(8,128)}, u32[]{:S(2)}, u32[]{:S(2)}) collective-permute-start(f32[2048,1024]{1,0:T(8,128)} %get-tuple-element.145), channel_id=1, source_target_pairs={{0,1},{1,0},{2,3},{3,2},{4,5},{5,4},{6,7},{7,6}} | collective-permute-start | bytes 25165832 | tf_op jit(solution)/shard_map/ppermute | solution.py:593
  714.7 36.1 %collective-permute-start.19 = (bf16[192,2048]{1,0:T(8,128)(2,1)}, bf16[192,2048]{1,0:T(8,128)(2,1)S(1)}, u32[]{:S(2)}, u32[]{:S(2)}) collective-permute-start(bf16[192,2048]{1,0:T(8,128)(2,1)} %get-tuple-element.110.refs_15_), channel_id=1, source_target_pairs={{0,3},{1,2},{2,1},{3,0},{4,7},{5,6},{6,5},{7,4}} | collective-permute-start | bytes 2359304 | tf_op jit(solution)/shard_map/ppermute | solution.py:593
  716.2 302.9 %collective-permute-start.29 = (f32[1024,2048]{1,0:T(8,128)}, f32[1024,2048]{1,0:T(8,128)}, u32[]{:S(2)}, u32[]{:S(2)}) collective-permute-start(f32[1024,2048]{1,0:T(8,128)} %get-tuple-element.143), channel_id=1, source_target_pairs={{0,1},{1,0},{2,3},{3,2},{4,5},{5,4},{6,7},{7,6}} | collective-permute-start | bytes 25165832 | tf_op jit(solution)/shard_map/ppermute | solution.py:593
  716.5 35.1 %collective-permute-start.10 = (bf16[192,2048]{1,0:T(8,128)(2,1)}, bf16[192,2048]{1,0:T(8,128)(2,1)S(1)}, u32[]{:S(2)}, u32[]{:S(2)}) collective-permute-start(bf16[192,2048]{1,0:T(8,128)(2,1)} %get-tuple-element.101.refs_6_), channel_id=1, source_target_pairs={{0,1},{1,0},{2,3},{3,2},{4,5},{5,4},{6,7},{7,6}} | collective-permute-start | bytes 2359304 | tf_op jit(solution)/shard_map/ppermute | solution.py:593
  735.0 33.7 %collective-permute-start.14 = (bf16[192,2048]{1,0:T(8,128)(2,1)}, bf16[192,2048]{1,0:T(8,128)(2,1)S(1)}, u32[]{:S(2)}, u32[]{:S(2)}) collective-permute-start(bf16[192,2048]{1,0:T(8,128)(2,1)} %get-tuple-element.105.refs_10_), channel_id=1, source_target_pairs={{0,2},{1,3},{2,0},{3,1},{4,6},{5,7},{6,4},{7,5}} | collective-permute-start | bytes 2359304 | tf_op jit(solution)/shard_map/ppermute | solution.py:593
  750.8 33.7 %collective-permute-start.18 = (bf16[192,2048]{1,0:T(8,128)(2,1)}, bf16[192,2048]{1,0:T(8,128)(2,1)S(1)}, u32[]{:S(2)}, u32[]{:S(2)}) collective-permute-start(bf16[192,2048]{1,0:T(8,128)(2,1)} %get-tuple-element.109.refs_14_), channel_id=1, source_target_pairs={{0,3},{1,2},{2,1},{3,0},{4,7},{5,6},{6,5},{7,4}} | collective-permute-start | bytes 2359304 | tf_op jit(solution)/shard_map/ppermute | solution.py:593
  751.6 50.8 %collective-permute-start.13 = (bf16[192,2048]{1,0:T(8,128)(2,1)}, bf16[192,2048]{1,0:T(8,128)(2,1)S(1)}, u32[]{:S(2)}, u32[]{:S(2)}) collective-permute-start(bf16[192,2048]{1,0:T(8,128)(2,1)} %get-tuple-element.104.refs_9_), channel_id=1, source_target_pairs={{0,2},{1,3},{2,0},{3,1},{4,6},{5,7},{6,4},{7,5}} | collective-permute-start | bytes 2359304 | tf_op jit(solution)/shard_map/ppermute | solution.py:593
  768.7 163.7 %collective-permute-start.24 = (f32[768,1024]{1,0:T(8,128)}, f32[768,1024]{1,0:T(8,128)}, u32[]{:S(2)}, u32[]{:S(2)}) collective-permute-start(f32[768,1024]{1,0:T(8,128)} %get-tuple-element.140), channel_id=1, source_target_pairs={{0,2},{1,3},{2,0},{3,1},{4,6},{5,7},{6,4},{7,5}} | collective-permute-start | bytes 9437192 | tf_op jit(solution)/shard_map/ppermute | solution.py:593
  784.5 101.1 %collective-permute-start.17 = (bf16[192,2048]{1,0:T(8,128)(2,1)}, bf16[192,2048]{1,0:T(8,128)(2,1)S(1)}, u32[]{:S(2)}, u32[]{:S(2)}) collective-permute-start(bf16[192,2048]{1,0:T(8,128)(2,1)} %get-tuple-element.108.refs_13_), channel_id=1, source_target_pairs={{0,3},{1,2},{2,1},{3,0},{4,7},{5,6},{6,5},{7,4}} | collective-permute-start | bytes 2359304 | tf_op jit(solution)/shard_map/ppermute | solution.py:593
  802.4 83.5 %collective-permute-start.9 = (bf16[192,2048]{1,0:T(8,128)(2,1)}, bf16[192,2048]{1,0:T(8,128)(2,1)S(1)}, u32[]{:S(2)}, u32[]{:S(2)}) collective-permute-start(bf16[192,2048]{1,0:T(8,128)(2,1)} %get-tuple-element.100.refs_5_), channel_id=1, source_target_pairs={{0,1},{1,0},{2,3},{3,2},{4,5},{5,4},{6,7},{7,6}} | collective-permute-start | bytes 2359304 | tf_op jit(solution)/shard_map/ppermute | solution.py:593
  885.8 36.0 %collective-permute-start.16 = (bf16[192,2048]{1,0:T(8,128)(2,1)}, bf16[192,2048]{1,0:T(8,128)(2,1)S(1)}, u32[]{:S(2)}, u32[]{:S(2)}) collective-permute-start(bf16[192,2048]{1,0:T(8,128)(2,1)} %get-tuple-element.107.refs_12_), channel_id=1, source_target_pairs={{0,3},{1,2},{2,1},{3,0},{4,7},{5,6},{6,5},{7,4}} | collective-permute-start | bytes 2359304 | tf_op jit(solution)/shard_map/ppermute | solution.py:593
  922.3 25.3 %collective-permute-start.27 = (f32[256,1024]{1,0:T(8,128)}, f32[256,1024]{1,0:T(8,128)S(1)}, u32[]{:S(2)}, u32[]{:S(2)}) collective-permute-start(f32[256,1024]{1,0:T(8,128)} %get-tuple-element.141), channel_id=1, source_target_pairs={{0,2},{1,3},{2,0},{3,1},{4,6},{5,7},{6,4},{7,5}} | collective-permute-start | bytes 3145736 | tf_op jit(solution)/shard_map/ppermute | solution.py:593
  924.9 73.2 %collective-permute-start.23 = (f32[768,1024]{1,0:T(8,128)}, f32[768,1024]{1,0:T(8,128)}, u32[]{:S(2)}, u32[]{:S(2)}) collective-permute-start(f32[768,1024]{1,0:T(8,128)} %get-tuple-element.140), channel_id=1, source_target_pairs={{0,1},{1,0},{2,3},{3,2},{4,5},{5,4},{6,7},{7,6}} | collective-permute-start | bytes 9437192 | tf_op jit(solution)/shard_map/ppermute | solution.py:593
  932.4 73.9 %collective-permute-start.25 = (f32[768,1024]{1,0:T(8,128)}, f32[768,1024]{1,0:T(8,128)}, u32[]{:S(2)}, u32[]{:S(2)}) collective-permute-start(f32[768,1024]{1,0:T(8,128)} %collective-permute-done.24), channel_id=1, source_target_pairs={{0,1},{1,0},{2,3},{3,2},{4,5},{5,4},{6,7},{7,6}} | collective-permute-start | bytes 9437192 | tf_op jit(solution)/shard_map/ppermute | solution.py:593
  947.6 49.4 %collective-permute-start.28 = (f32[256,1024]{1,0:T(8,128)S(1)}, f32[256,1024]{1,0:T(8,128)S(1)}, u32[]{:S(2)}, u32[]{:S(2)}) collective-permute-start(f32[256,1024]{1,0:T(8,128)S(1)} %collective-permute-done.27), channel_id=1, source_target_pairs={{0,1},{1,0},{2,3},{3,2},{4,5},{5,4},{6,7},{7,6}} | collective-permute-start | bytes 3145736 | tf_op jit(solution)/shard_map/ppermute | solution.py:593
  (38 other events, 2656.6 us)
